TPU v7x, 32 devices: a whole 2x2x4 slice. The times are simulated.
32 devices in a mesh: gx: 2 (over core), gy: 4 (over y, x), gz: 4 (over z).
Axes of the slice: x: 2, y: 2, z: 4, core: 2. Of those that a mesh axis runs over, the one named last changes fastest.
Arguments:
- queries: bfloat16 [128, 32, 128], P(None, 'gy'), may hold values from -6 to 6
- passages: bfloat16 [1024, 256, 128], P('gx', 'gz'), may hold values from -0.5 to 0.5
- passage_len: int32 [1024], P('gx'), may hold values from 32 to 256
- query_len: int32 [128], replicated, may hold values from 8 to 32
Outputs:
- log_probs: float32 [128, 1024], P(None, ('gx', 'gz'))
All inputs are finite; a program needn't handle non-finite values.
Results may differ from a plain program's by a relative error of at most 0.0003.
Values sent between devices are 32-bit elements; how exact they have to be, the bound alone decides.
No kernel may reach another device: no remote copies, remote signals or barrier semaphores. Data moves between devices by JAX's collectives and lax.ppermute only.
A program may use at most 64 MiB of HBM per device.

v0:
```python
import math

import jax
import jax.numpy as jnp
from jax import lax
from jax.sharding import PartitionSpec as P

masked_low = -1e30


def combined_all(array, axis, combine):
    everything = jax.tree.map(lambda part: lax.all_gather(part, axis), array)
    initial = jax.tree.map(lambda part: part[0], everything)

    def turn(k, so_far):
        return combine(so_far, jax.tree.map(lambda part: part[k], everything))

    return lax.fori_loop(1, lax.axis_size(axis), turn, initial)


def token_maxima(queries, passages, passage_len):
    query_count = queries.shape[0]
    query_rows = queries.shape[1]
    width = queries.shape[2]
    passage_count = passages.shape[0]
    token_count = passages.shape[1]
    flat_queries = queries.reshape(query_count * query_rows, width)
    per_block = math.gcd(passage_count, 32)
    num_blocks = passage_count // per_block
    token_ids = lax.axis_index("gz") * token_count + jnp.arange(token_count, dtype=jnp.int32)
    tile_stack = passages.reshape(num_blocks, per_block * token_count, width)
    length_stack = passage_len.reshape(num_blocks, per_block)

    def block_maxima(packed):
        passage_tile, tile_len = packed
        scores = lax.dot_general(
            flat_queries, passage_tile, (((1,), (1,)), ((), ())), preferred_element_type=jnp.float32
        )
        scores = scores.reshape(query_count * query_rows, per_block, token_count)
        usable = token_ids[None, :] < tile_len[:, None]
        scores = jnp.where(usable[None], scores, masked_low)
        return jnp.max(scores, axis=2)

    pieces = lax.map(block_maxima, (tile_stack, length_stack))
    return jnp.transpose(pieces, (1, 0, 2)).reshape(query_count, query_rows, passage_count)


def join_pairs(earlier, other_pair):
    highest = jnp.maximum(earlier[0], other_pair[0])
    summed = earlier[1] * jnp.exp(earlier[0] - highest) + other_pair[1] * jnp.exp(
        other_pair[0] - highest
    )
    return (highest, summed)


def fold_peers(received):
    return jnp.max(received, axis=2)


def shards(queries, passages, passage_len, query_len):
    maxima = token_maxima(queries, passages, passage_len)
    query_count = maxima.shape[0]
    query_rows = maxima.shape[1]
    passage_count = maxima.shape[2]
    query_ids = lax.axis_index("gy") * query_rows + jnp.arange(query_rows, dtype=jnp.int32)
    counted = (query_ids[None, :] < query_len[:, None])[:, :, None]
    spread = maxima.reshape(query_count, query_rows, 1, passage_count)
    merged = fold_peers(lax.all_to_all(spread, "gz", split_axis=3, concat_axis=2, tiled=True))
    partial_value = jnp.sum(jnp.where(counted, merged, 0.0), axis=1)
    scores_here = lax.psum(partial_value, "gy")
    local_top = jnp.max(scores_here, axis=1)
    local_sum = jnp.sum(jnp.exp(scores_here - local_top[:, None]), axis=1)
    highest, summed = combined_all((local_top, local_sum), ("gx", "gz"), join_pairs)
    return scores_here - (highest + jnp.log(summed))[:, None]


def solution(mesh):
    return jax.shard_map(
        shards,
        mesh=mesh,
        in_specs=(P(None, "gy", None), P("gx", "gz", None), P("gx"), P()),
        out_specs=P(None, ("gx", "gz")),
        check_vma=False,
    )
```

profile of v0, /device:TPU:0, one launch (start us, length us, event | category | flops | bytes accessed | tf_op | source)
XLA Modules:
  0.0 207.8 jit_solution(13668500045373860605)
XLA Ops:
  6.5 0.8 reshape.79
  7.3 40.6 %while.29 = (s32[]{:T(128)}, f32[16,1024,32]{1,2,0:T(8,128)S(1)}, s32[16,32]{1,0:T(8,128)S(1)}, bf16[16,2048,128]{2,1,0:T(8,128)(2,1)}, bf16[1024,128]{1,0:T(8,128)(2,1)}, /*index=5*/s32[]{:T(128)}, s32[]{:T(128)}) while((s32[]{:T(128)}, f32[16,1024,32]{1,2,0:T(8,128)S(1)}, s32[16,32]{1,0:T(8,128)S(1)}, ...), condition=%wide.region_2.3_spmd.clone, body=%wide.region_0.2_spmd.clone.sunk | while | flops 541034560 | bytes 1185241 | solution.py:44
  7.3 0.1 broadcast_compare_fusion.3
  7.4 2.4 %select_reduce_fusion.3 = f32[1024,32]{0,1:T(8,128)S(1)} fusion(pred[32,64]{1,0:T(8,128)(4,1)S(1)} %broadcast_compare_fusion.3, bf16[1024,128]{1,0:T(8,128)(2,1)} %get-tuple-element.302, bf16[16,2048,128]{2,1,0:T(8,128)(2,1)} %get-tuple-element.301, s32[]{:T(128)} %get-tuple-element.291), kind=kOutput, calls=%fused_computation.7.clone.1 | convolution fusion | flops 541032448 | bytes 920064 | tf_op jit(solution)/shard_map/while/body/eval_jaxpr/dot_general | solution.py:36
  9.8 0.1 broadcast_compare_fusion.3
  9.9 2.4 %select_reduce_fusion.3 = f32[1024,32]{0,1:T(8,128)S(1)} fusion(pred[32,64]{1,0:T(8,128)(4,1)S(1)} %broadcast_compare_fusion.3, bf16[1024,128]{1,0:T(8,128)(2,1)} %get-tuple-element.302, bf16[16,2048,128]{2,1,0:T(8,128)(2,1)} %get-tuple-element.301, s32[]{:T(128)} %get-tuple-element.291), kind=kOutput, calls=%fused_computation.7.clone.1 | convolution fusion | flops 541032448 | bytes 920064 | tf_op jit(solution)/shard_map/while/body/eval_jaxpr/dot_general | solution.py:36
  12.4 0.1 broadcast_compare_fusion.3
  12.5 2.4 %select_reduce_fusion.3 = f32[1024,32]{0,1:T(8,128)S(1)} fusion(pred[32,64]{1,0:T(8,128)(4,1)S(1)} %broadcast_compare_fusion.3, bf16[1024,128]{1,0:T(8,128)(2,1)} %get-tuple-element.302, bf16[16,2048,128]{2,1,0:T(8,128)(2,1)} %get-tuple-element.301, s32[]{:T(128)} %get-tuple-element.291), kind=kOutput, calls=%fused_computation.7.clone.1 | convolution fusion | flops 541032448 | bytes 920064 | tf_op jit(solution)/shard_map/while/body/eval_jaxpr/dot_general | solution.py:36
  14.9 0.1 broadcast_compare_fusion.3
  15.0 2.4 %select_reduce_fusion.3 = f32[1024,32]{0,1:T(8,128)S(1)} fusion(pred[32,64]{1,0:T(8,128)(4,1)S(1)} %broadcast_compare_fusion.3, bf16[1024,128]{1,0:T(8,128)(2,1)} %get-tuple-element.302, bf16[16,2048,128]{2,1,0:T(8,128)(2,1)} %get-tuple-element.301, s32[]{:T(128)} %get-tuple-element.291), kind=kOutput, calls=%fused_computation.7.clone.1 | convolution fusion | flops 541032448 | bytes 920064 | tf_op jit(solution)/shard_map/while/body/eval_jaxpr/dot_general | solution.py:36
  17.5 0.1 broadcast_compare_fusion.3
  17.5 2.4 %select_reduce_fusion.3 = f32[1024,32]{0,1:T(8,128)S(1)} fusion(pred[32,64]{1,0:T(8,128)(4,1)S(1)} %broadcast_compare_fusion.3, bf16[1024,128]{1,0:T(8,128)(2,1)} %get-tuple-element.302, bf16[16,2048,128]{2,1,0:T(8,128)(2,1)} %get-tuple-element.301, s32[]{:T(128)} %get-tuple-element.291), kind=kOutput, calls=%fused_computation.7.clone.1 | convolution fusion | flops 541032448 | bytes 920064 | tf_op jit(solution)/shard_map/while/body/eval_jaxpr/dot_general | solution.py:36
  20.0 0.1 broadcast_compare_fusion.3
  20.1 2.4 %select_reduce_fusion.3 = f32[1024,32]{0,1:T(8,128)S(1)} fusion(pred[32,64]{1,0:T(8,128)(4,1)S(1)} %broadcast_compare_fusion.3, bf16[1024,128]{1,0:T(8,128)(2,1)} %get-tuple-element.302, bf16[16,2048,128]{2,1,0:T(8,128)(2,1)} %get-tuple-element.301, s32[]{:T(128)} %get-tuple-element.291), kind=kOutput, calls=%fused_computation.7.clone.1 | convolution fusion | flops 541032448 | bytes 920064 | tf_op jit(solution)/shard_map/while/body/eval_jaxpr/dot_general | solution.py:36
  22.5 0.1 broadcast_compare_fusion.3
  22.6 2.4 %select_reduce_fusion.3 = f32[1024,32]{0,1:T(8,128)S(1)} fusion(pred[32,64]{1,0:T(8,128)(4,1)S(1)} %broadcast_compare_fusion.3, bf16[1024,128]{1,0:T(8,128)(2,1)} %get-tuple-element.302, bf16[16,2048,128]{2,1,0:T(8,128)(2,1)} %get-tuple-element.301, s32[]{:T(128)} %get-tuple-element.291), kind=kOutput, calls=%fused_computation.7.clone.1 | convolution fusion | flops 541032448 | bytes 920064 | tf_op jit(solution)/shard_map/while/body/eval_jaxpr/dot_general | solution.py:36
  25.1 0.1 broadcast_compare_fusion.3
  25.2 2.4 %select_reduce_fusion.3 = f32[1024,32]{0,1:T(8,128)S(1)} fusion(pred[32,64]{1,0:T(8,128)(4,1)S(1)} %broadcast_compare_fusion.3, bf16[1024,128]{1,0:T(8,128)(2,1)} %get-tuple-element.302, bf16[16,2048,128]{2,1,0:T(8,128)(2,1)} %get-tuple-element.301, s32[]{:T(128)} %get-tuple-element.291), kind=kOutput, calls=%fused_computation.7.clone.1 | convolution fusion | flops 541032448 | bytes 920064 | tf_op jit(solution)/shard_map/while/body/eval_jaxpr/dot_general | solution.py:36
  27.6 0.1 broadcast_compare_fusion.3
  27.7 2.4 %select_reduce_fusion.3 = f32[1024,32]{0,1:T(8,128)S(1)} fusion(pred[32,64]{1,0:T(8,128)(4,1)S(1)} %broadcast_compare_fusion.3, bf16[1024,128]{1,0:T(8,128)(2,1)} %get-tuple-element.302, bf16[16,2048,128]{2,1,0:T(8,128)(2,1)} %get-tuple-element.301, s32[]{:T(128)} %get-tuple-element.291), kind=kOutput, calls=%fused_computation.7.clone.1 | convolution fusion | flops 541032448 | bytes 920064 | tf_op jit(solution)/shard_map/while/body/eval_jaxpr/dot_general | solution.py:36
  30.2 0.1 broadcast_compare_fusion.3
  30.2 2.4 %select_reduce_fusion.3 = f32[1024,32]{0,1:T(8,128)S(1)} fusion(pred[32,64]{1,0:T(8,128)(4,1)S(1)} %broadcast_compare_fusion.3, bf16[1024,128]{1,0:T(8,128)(2,1)} %get-tuple-element.302, bf16[16,2048,128]{2,1,0:T(8,128)(2,1)} %get-tuple-element.301, s32[]{:T(128)} %get-tuple-element.291), kind=kOutput, calls=%fused_computation.7.clone.1 | convolution fusion | flops 541032448 | bytes 920064 | tf_op jit(solution)/shard_map/while/body/eval_jaxpr/dot_general | solution.py:36
  32.7 0.1 broadcast_compare_fusion.3
  32.8 2.4 %select_reduce_fusion.3 = f32[1024,32]{0,1:T(8,128)S(1)} fusion(pred[32,64]{1,0:T(8,128)(4,1)S(1)} %broadcast_compare_fusion.3, bf16[1024,128]{1,0:T(8,128)(2,1)} %get-tuple-element.302, bf16[16,2048,128]{2,1,0:T(8,128)(2,1)} %get-tuple-element.301, s32[]{:T(128)} %get-tuple-element.291), kind=kOutput, calls=%fused_computation.7.clone.1 | convolution fusion | flops 541032448 | bytes 920064 | tf_op jit(solution)/shard_map/while/body/eval_jaxpr/dot_general | solution.py:36
  35.2 0.1 broadcast_compare_fusion.3
  35.3 2.4 %select_reduce_fusion.3 = f32[1024,32]{0,1:T(8,128)S(1)} fusion(pred[32,64]{1,0:T(8,128)(4,1)S(1)} %broadcast_compare_fusion.3, bf16[1024,128]{1,0:T(8,128)(2,1)} %get-tuple-element.302, bf16[16,2048,128]{2,1,0:T(8,128)(2,1)} %get-tuple-element.301, s32[]{:T(128)} %get-tuple-element.291), kind=kOutput, calls=%fused_computation.7.clone.1 | convolution fusion | flops 541032448 | bytes 920064 | tf_op jit(solution)/shard_map/while/body/eval_jaxpr/dot_general | solution.py:36
  37.8 0.1 broadcast_compare_fusion.3
  37.8 2.4 %select_reduce_fusion.3 = f32[1024,32]{0,1:T(8,128)S(1)} fusion(pred[32,64]{1,0:T(8,128)(4,1)S(1)} %broadcast_compare_fusion.3, bf16[1024,128]{1,0:T(8,128)(2,1)} %get-tuple-element.302, bf16[16,2048,128]{2,1,0:T(8,128)(2,1)} %get-tuple-element.301, s32[]{:T(128)} %get-tuple-element.291), kind=kOutput, calls=%fused_computation.7.clone.1 | convolution fusion | flops 541032448 | bytes 920064 | tf_op jit(solution)/shard_map/while/body/eval_jaxpr/dot_general | solution.py:36
  40.3 0.1 broadcast_compare_fusion.3
  40.4 2.4 %select_reduce_fusion.3 = f32[1024,32]{0,1:T(8,128)S(1)} fusion(pred[32,64]{1,0:T(8,128)(4,1)S(1)} %broadcast_compare_fusion.3, bf16[1024,128]{1,0:T(8,128)(2,1)} %get-tuple-element.302, bf16[16,2048,128]{2,1,0:T(8,128)(2,1)} %get-tuple-element.301, s32[]{:T(128)} %get-tuple-element.291), kind=kOutput, calls=%fused_computation.7.clone.1 | convolution fusion | flops 541032448 | bytes 920064 | tf_op jit(solution)/shard_map/while/body/eval_jaxpr/dot_general | solution.py:36
  42.8 0.1 broadcast_compare_fusion.3
  42.9 2.4 %select_reduce_fusion.3 = f32[1024,32]{0,1:T(8,128)S(1)} fusion(pred[32,64]{1,0:T(8,128)(4,1)S(1)} %broadcast_compare_fusion.3, bf16[1024,128]{1,0:T(8,128)(2,1)} %get-tuple-element.302, bf16[16,2048,128]{2,1,0:T(8,128)(2,1)} %get-tuple-element.301, s32[]{:T(128)} %get-tuple-element.291), kind=kOutput, calls=%fused_computation.7.clone.1 | convolution fusion | flops 541032448 | bytes 920064 | tf_op jit(solution)/shard_map/while/body/eval_jaxpr/dot_general | solution.py:36
  45.4 0.1 broadcast_compare_fusion.3
  45.5 2.4 %select_reduce_fusion.3 = f32[1024,32]{0,1:T(8,128)S(1)} fusion(pred[32,64]{1,0:T(8,128)(4,1)S(1)} %broadcast_compare_fusion.3, bf16[1024,128]{1,0:T(8,128)(2,1)} %get-tuple-element.302, bf16[16,2048,128]{2,1,0:T(8,128)(2,1)} %get-tuple-element.301, s32[]{:T(128)} %get-tuple-element.291), kind=kOutput, calls=%fused_computation.7.clone.1 | convolution fusion | flops 541032448 | bytes 920064 | tf_op jit(solution)/shard_map/while/body/eval_jaxpr/dot_general | solution.py:36
  47.9 6.2 %copy.11 = f32[1024,16,32]{2,1,0:T(8,128)} copy(f32[1024,16,32]{0,2,1:T(8,128)S(1)} %bitcast.51) | data formatting | bytes 4194304 | tf_op jit(solution)/shard_map/transpose | solution.py:45
  54.1 6.2 %reshape_reshape.3 = f32[128,8,1,512]{3,1,0,2:T(8,128)S(1)} reshape(f32[1024,16,32]{2,1,0:T(8,128)} %copy.11) | data formatting | bytes 4194304 | tf_op jit(solution)/shard_map/reshape;reshape | solution.py:67
  60.4 2.1 %copy.12 = f32[128,8,1,512]{0,1,2,3:T(8,128)} copy(f32[128,8,1,512]{3,1,0,2:T(8,128)S(1)} %reshape_reshape.3) | data formatting | bytes 4194304 | tf_op jit(solution)/shard_map/reshape;reshape | solution.py:67
  62.5 0.0 copy-start
  62.5 6.5 %all-to-all-start = ((f32[128,8,1,512]{0,1,2,3:T(8,128)}), f32[128,8,1,512]{0,1,2,3:T(8,128)S(1)}, u32[]{:S(2)}, u32[]{:S(2)}) async-start(f32[128,8,1,512]{0,1,2,3:T(8,128)} %copy.12), calls=%async_computation | async-start | bytes 4194304 | tf_op jit(solution)/shard_map/all_to_all | solution.py:68
  68.9 0.0 all-reduce.2.cloned.1.call-start
  68.9 0.0 copy-done
  69.0 0.1 broadcast_compare_fusion.1
  69.0 48.1 %all-to-all-done = f32[128,8,1,512]{0,1,2,3:T(8,128)S(1)} async-done(((f32[128,8,1,512]{0,1,2,3:T(8,128)}), f32[128,8,1,512]{0,1,2,3:T(8,128)S(1)}, u32[]{:S(2)}, u32[]{:S(2)}) %all-to-all-start) | async-done | bytes 2097184 | tf_op jit(solution)/shard_map/all_to_all | solution.py:68
  117.1 0.2 reduce_max.27
  117.3 4.8 %copy.15 = f32[128,8,128]{1,0,2:T(8,128)} copy(f32[128,8,128]{0,1,2:T(8,128)S(1)} %reduce_max.27) | data formatting | bytes 1048576
  122.2 6.2 %select_reduce_fusion.1 = f32[128,128]{0,1:T(8,128)} fusion(f32[128,8,128]{1,0,2:T(8,128)} %copy.15, pred[128,8]{1,0:T(8,128)(4,1)S(1)} %broadcast_compare_fusion.1), kind=kLoop, calls=%fused_computation.17 | loop fusion | flops 245760 | bytes 590848 | tf_op jit(solution)/shard_map/reduce_sum | solution.py:69
  128.4 0.0 all-reduce.2.cloned.1.call-update
  128.4 41.1 %all-reduce.2.cloned.1.call-done = f32[128,128]{0,1:T(8,128)} async-done(((f32[128,128]{0,1:T(8,128)}), f32[128,128]{0,1:T(8,128)}) %all-reduce.2.cloned.1.call-update) | async-done | bytes 65552 | tf_op jit(solution)/shard_map/psum | solution.py:70
  169.5 0.9 reduce_max.28
  170.4 0.9 exponential_reduce_fusion
  171.3 15.1 %all-gather.3 = f32[8,1,128]{2,1,0:T(1,128)S(1)} all-gather(f32[1,1,128]{2,1,0:T(1,128)S(1)} %bitcast.55), channel_id=3, replica_groups=mesh['gx'=2,'gy'=4,'gz'=4] {'gx','gz'}, dimensions={0}, use_global_device_ids=true | all-gather | bytes 4608 | tf_op jit(solution)/shard_map/all_gather | solution.py:12
  186.3 12.8 %all-gather.2 = f32[8,1,128]{2,1,0:T(1,128)S(1)} all-gather(f32[1,1,128]{2,1,0:T(1,128)S(1)} %bitcast.54), channel_id=2, replica_groups=mesh['gx'=2,'gy'=4,'gz'=4] {'gx','gz'}, dimensions={0}, use_global_device_ids=true | all-gather | bytes 4608 | tf_op jit(solution)/shard_map/all_gather | solution.py:12
  199.1 0.3 while.28
  199.4 0.8 broadcast_subtract_fusion
  200.3 0.7 copy.14
  (60 shorter events, 0.7 us)
Async XLA Ops:
  62.5 6.5 %copy-start = (s32[128]{0:T(128)S(1)}, s32[128]{0:T(128)}, u32[]{:S(2)}) copy-start(s32[128]{0:T(128)} %param.11) | copy-start | bytes 1540
  62.5 54.7 %all-to-all-start = ((f32[128,8,1,512]{0,1,2,3:T(8,128)}), f32[128,8,1,512]{0,1,2,3:T(8,128)S(1)}, u32[]{:S(2)}, u32[]{:S(2)}) async-start(f32[128,8,1,512]{0,1,2,3:T(8,128)} %copy.12), calls=%async_computation | async-start | bytes 4194304 | tf_op jit(solution)/shard_map/all_to_all | solution.py:68
  68.9 100.6 %all-reduce.2.cloned.1.call-start = ((), (), s32[]{:S(2)}) async-start(), calls=%async_computation.1 | async-start | bytes 131072 | tf_op jit(solution)/shard_map/psum | solution.py:70
Sparse Core Ops, SparseCore 0:
  128.5 40.9 all-reduce.1
where the time goes:
time: 209 us; the launch traced here: 208 us
  waiting for transfers between devices  89.2 us (43%)
  matrix products  38.2 us (18%)
  blocking collectives  27.8 us (13%)
  local copies, waits for them, and re-layouts  21.3 us (10%)
  between operations  13.4 us (6%)
  other arithmetic  10.6 us (5%)
  starting transfers between devices  6.48 us (3%)
    all_to_all x1, waiting for transfers between devices, shards(): lax.all_to_all(spread, 'gz', split_axis=3, concat_axis=2, tiled=True)  48.1 us
    psum x1, waiting for transfers between devices, shards(): scores_here = lax.psum(partial_value, 'gy')  41.1 us
    dot_general x16, matrix products, block_maxima(): lax.dot_general(flat_queries, passage_tile, (((1,), (1,)), ((), ())), pre...  38.2 us
    all_gather x2, blocking collectives, combined_all(): everything = jax.tree.map(lambda part: lax.all_gather(part, axis), array)  27.8 us
    another operation x2, local copies, waits for them, and re-layouts, shards(): spread = maxima.reshape(query_count, query_rows, 1, passage_count)  8.32 us
    all_to_all x1, starting transfers between devices, shards(): lax.all_to_all(spread, 'gz', split_axis=3, concat_axis=2, tiled=True)  6.48 us
    reduce_sum x1, other arithmetic, shards(): partial_value = jnp.sum(jnp.where(counted, merged, 0.0), axis=1)  6.25 us
    transpose x1, local copies, waits for them, and re-layouts, token_maxima(): jnp.transpose(pieces, (1, 0, 2))  6.23 us
  transfers between devices with their start and end apart: 2, of which 2 were waited for; matrix products, arithmetic and copies ran while one was open for 0% of the time, Pallas kernels for 0%

commit v1 on v0

v1 whole, which is shorter than its diff:
```python
import functools

import jax
import jax.numpy as jnp
from jax import lax
from jax.experimental import pallas as pl
from jax.experimental.pallas import tpu as pltpu
from jax.sharding import PartitionSpec as P

masked_low = -1e30


def maxima_kernel(start_ref, len_ref, queries_ref, passages_ref, out_ref, *, rows_at_once, columns):
    passage_block, token_count, width = passages_ref.shape
    query_rows = queries_ref.shape[0]
    per_dot = rows_at_once // token_count
    first = start_ref[0] + pl.program_id(0) * passage_block
    token_ids = lax.broadcasted_iota(jnp.int32, (token_count, columns), 0)
    for m in range(passage_block // per_dot):
        tile = passages_ref[m * per_dot : (m + 1) * per_dot].reshape(per_dot * token_count, width)
        for j in range(query_rows // columns):
            scores = lax.dot_general(
                tile,
                queries_ref[j * columns : (j + 1) * columns],
                (((1,), (1,)), ((), ())),
                preferred_element_type=jnp.float32,
            )
            best = []
            for k in range(per_dot):
                usable = token_ids < len_ref[first + m * per_dot + k]
                mine = jnp.where(usable, scores[k * token_count : (k + 1) * token_count], masked_low)
                best.append(jnp.max(mine, axis=0, keepdims=True))
            out_ref[m * per_dot : (m + 1) * per_dot, j * columns : (j + 1) * columns] = (
                jnp.concatenate(best, axis=0)
            )


def block_maxima(flat_queries, passages, usable_tokens, block, block_size):
    passage_count, token_count, width = passages.shape
    query_rows = flat_queries.shape[0]
    step = min(64, block_size)
    steps = block_size // step
    return pl.pallas_call(
        functools.partial(
            maxima_kernel,
            rows_at_once=min(step, max(1, 1024 // token_count)) * token_count,
            columns=min(256, query_rows),
        ),
        grid_spec=pltpu.PrefetchScalarGridSpec(
            num_scalar_prefetch=2,
            grid=(steps,),
            in_specs=[
                pl.BlockSpec((query_rows, width), lambda i, start, lens: (0, 0)),
                pl.BlockSpec(
                    (step, token_count, width), lambda i, start, lens: (start[0] // step + i, 0, 0)
                ),
            ],
            out_specs=pl.BlockSpec((step, query_rows), lambda i, start, lens: (i, 0)),
        ),
        out_shape=jax.ShapeDtypeStruct((block_size, query_rows), jnp.float32),
        cost_estimate=pl.CostEstimate(
            flops=2 * 2 * block_size * token_count * query_rows * width,
            bytes_accessed=block_size * (token_count * width * 2 + query_rows * 4),
            transcendentals=0,
        ),
        name="maxima",
    )((block * block_size).reshape(1), usable_tokens, flat_queries, passages)


def exchange(array, axis, distance):
    size = lax.axis_size(axis)
    return lax.ppermute(array, axis, [(k, k ^ distance) for k in range(size)])


def hypercube(array, axis, combine):
    distance = 1
    while distance < lax.axis_size(axis):
        array = combine(array, exchange(array, axis, distance))
        distance *= 2
    return array


def join_pairs(one, other):
    top = jnp.maximum(one[0], other[0])
    summed = one[1] * jnp.exp(one[0] - top) + other[1] * jnp.exp(other[0] - top)
    return jnp.stack([top, summed])


def shards(queries, passages, passage_len, query_len):
    query_count, query_rows, width = queries.shape
    passage_count, token_count, _ = passages.shape
    gz = lax.axis_index("gz")
    owners = lax.axis_size("gz")
    block_size = passage_count // owners
    flat_queries = jnp.transpose(queries, (1, 0, 2)).reshape(query_rows * query_count, width)
    usable_tokens = passage_len - gz * token_count

    merged = None
    arrived = []
    for distance in range(owners - 1, -1, -1):
        block = block_maxima(flat_queries, passages, usable_tokens, gz ^ distance, block_size)
        arrived.append(exchange(block, "gz", distance) if distance else block)
    merged = functools.reduce(jnp.maximum, arrived)
    query_ids = lax.axis_index("gy") * query_rows + jnp.arange(query_rows, dtype=jnp.int32)
    counted = query_ids[:, None] < query_len[None, :]
    partial_value = jnp.sum(
        jnp.where(counted[None], merged.reshape(block_size, query_rows, query_count), 0.0), axis=1
    )
    scores = hypercube(partial_value, "gy", jnp.add)
    top = jnp.max(scores, axis=0)
    summed = jnp.sum(jnp.exp(scores - top[None]), axis=0)
    pair = jnp.stack([top, summed])
    pair = hypercube(pair, "gx", join_pairs)
    pair = hypercube(pair, "gz", join_pairs)
    return jnp.transpose(scores - (pair[0] + jnp.log(pair[1]))[None])


def solution(mesh):
    return jax.shard_map(
        shards,
        mesh=mesh,
        in_specs=(P(None, "gy", None), P("gx", "gz", None), P("gx"), P()),
        out_specs=P(None, ("gx", "gz")),
        check_vma=False,
    )
```

time: 209 us -> 81.3 us (0.39)
  waiting for transfers between devices: 89.2 us -> 35.7 us
  matrix products: 38.2 us -> 0 us
  Pallas kernels: 0 us -> 29.8 us
  blocking collectives: 27.8 us -> 0 us
  local copies, waits for them, and re-layouts: 21.3 us -> 2.54 us
  between operations: 13.4 us -> 0.07 us
  other arithmetic: 10.6 us -> 2.84 us
  starting transfers between devices: 6.48 us -> 9.88 us
    all_to_all x1 -> x0, waiting for transfers between devices: 48.1 us -> none  [shards(): lax.all_to_all(spread, 'gz', split_axis=3, concat_axis=2, tiled=True)]
    psum x1 -> x0, waiting for transfers between devices: 41.1 us -> none  [shards(): scores_here = lax.psum(partial_value, 'gy')]
    dot_general x16 -> x0, matrix products: 38.2 us -> none  [block_maxima(): lax.dot_general(flat_queries, passage_tile, (((1,), (1,)), ((), ())), pre...]
    ppermute x0 -> x8, waiting for transfers between devices: none -> 35.7 us  [exchange(): return lax.ppermute(array, axis, [(k, k ^ distance) for k in range(size)])]
    pallas_call x0 -> x4, Pallas kernels: none -> 29.8 us  [block_maxima(): pl.pallas_call(functools.partial(maxima_kernel, rows_at_once=min(step, ma...]
    all_gather x2 -> x0, blocking collectives: 27.8 us -> none  [combined_all(): everything = jax.tree.map(lambda part: lax.all_gather(part, axis), array)]
    ppermute x0 -> x8, starting transfers between devices: none -> 9.88 us  [exchange(): return lax.ppermute(array, axis, [(k, k ^ distance) for k in range(size)])]
    another operation x2 -> x0, local copies, waits for them, and re-layouts: 8.32 us -> none  [shards(): spread = maxima.reshape(query_count, query_rows, 1, passage_count)]
  transfers between devices with their start and end apart: 2 -> 8, of which waited for: 2 -> 6; matrix products, arithmetic and copies ran while one was open for 0% -> 0% of each run, Pallas kernels for 0% -> 28%
where the time goes in v1:
time: 81.3 us; the launch traced here: 80.9 us
  waiting for transfers between devices  35.7 us (44%)
  Pallas kernels  29.8 us (37%)
  starting transfers between devices  9.88 us (12%)
  other arithmetic  2.84 us (3%)
  local copies, waits for them, and re-layouts  2.54 us (3%)
    ppermute x8, waiting for transfers between devices, exchange(): return lax.ppermute(array, axis, [(k, k ^ distance) for k in range(size)])  35.7 us
    pallas_call x4, Pallas kernels, block_maxima(): pl.pallas_call(functools.partial(maxima_kernel, rows_at_once=min(step, ma...  29.8 us
    ppermute x8, starting transfers between devices, exchange(): return lax.ppermute(array, axis, [(k, k ^ distance) for k in range(size)])  9.88 us
    transpose x1, local copies, waits for them, and re-layouts, shards(): jnp.transpose(queries, (1, 0, 2)).reshape(query_rows * query_count, width)  1.7 us
  transfers between devices with their start and end apart: 8, of which 6 were waited for; matrix products, arithmetic and copies ran while one was open for 0% of the time, Pallas kernels for 28%

profile of v1, /device:TPU:0, one launch (start us, length us, event | category | flops | bytes accessed | tf_op | source)
XLA Modules:
  0.0 80.9 jit_solution(12297461548013489188)
XLA Ops:
  0.0 1.7 %copy.6 = bf16[8,128,128]{2,1,0:T(8,128)(2,1)} copy(bf16[8,128,128]{2,0,1:T(8,128)(2,1)} %bitcast.22) | data formatting | bytes 524288 | tf_op jit(solution)/shard_map/transpose | solution.py:95
  1.7 1.3 %broadcast_subtract_fusion.len_ref = s32[512]{0:T(512)} fusion(s32[512]{0:T(512)} %param.6, s32[]{:T(128)S(6)} %mul.50), kind=kLoop, calls=%fused_computation.9 | loop fusion | flops 512 | bytes 4100 | tf_op jit(solution)/shard_map/sub | solution.py:96
  3.0 7.4 %maxima.4 = f32[128,1024]{1,0:T(8,128)} custom-call(s32[1]{0:T(128)} %bitcast.start_ref, s32[512]{0:T(512)} %broadcast_subtract_fusion.len_ref, bf16[1024,128]{1,0:T(8,128)(2,1)} %bitcast.23, bf16[512,64,128]{2,1,0:T(8,128)(2,1)} %passages_ref.7), custom_call_target="tpu_custom_call" | custom-call | flops 4294967296 | bytes 2621440 | tf_op jit(solution)/shard_map/maxima/pallas_call | solution.py:43
  10.4 5.1 %collective-permute-start = (f32[128,1024]{1,0:T(8,128)}, f32[128,1024]{1,0:T(8,128)S(1)}, u32[]{:S(2)}, u32[]{:S(2)}) collective-permute-start(f32[128,1024]{1,0:T(8,128)} %maxima.4), channel_id=1, source_target_pairs={{0,3},{1,2},{2,1},{3,0},{4,7},{5,6},{6,5},{7,4},{8,11},{9,10},{10,... | collective-permute-start | bytes 1572872 | tf_op jit(solution)/shard_map/ppermute | solution.py:72
  15.5 7.4 %maxima.5 = f32[128,1024]{1,0:T(8,128)} custom-call(s32[1]{0:T(128)} %bitcast.3.start_ref, s32[512]{0:T(512)} %broadcast_subtract_fusion.len_ref, bf16[1024,128]{1,0:T(8,128)(2,1)} %bitcast.24, bf16[512,64,128]{2,1,0:T(8,128)(2,1)} %passages_ref.7), custom_call_target="tpu_custom_call" | custom-call | flops 4294967296 | bytes 2621440 | tf_op jit(solution)/shard_map/maxima/pallas_call | solution.py:43
  22.9 0.0 copy-start
  22.9 0.0 collective-permute-start.1
  22.9 7.6 %maxima.6 = f32[128,1024]{1,0:T(8,128)} custom-call(s32[1]{0:T(128)} %bitcast.4.start_ref, s32[512]{0:T(512)} %broadcast_subtract_fusion.len_ref, bf16[1024,128]{1,0:T(8,128)(2,1)} %bitcast.25, bf16[512,64,128]{2,1,0:T(8,128)(2,1)} %passages_ref.7), custom_call_target="tpu_custom_call" | custom-call | flops 4294967296 | bytes 2621440 | tf_op jit(solution)/shard_map/maxima/pallas_call | solution.py:43
  30.5 0.4 collective-permute-start.2
  30.9 0.0 copy-done
  30.9 0.1 broadcast_compare_fusion
  31.0 7.4 %maxima.7 = f32[128,1024]{1,0:T(8,128)} custom-call(s32[1]{0:T(128)} %bitcast.5.start_ref, s32[512]{0:T(512)} %broadcast_subtract_fusion.len_ref, bf16[1024,128]{1,0:T(8,128)(2,1)} %bitcast.26, bf16[512,64,128]{2,1,0:T(8,128)(2,1)} %passages_ref.7), custom_call_target="tpu_custom_call" | custom-call | flops 4294967296 | bytes 2621440 | tf_op jit(solution)/shard_map/maxima/pallas_call | solution.py:43
  38.4 0.0 collective-permute-done
  38.4 22.0 %collective-permute-done.1 = f32[128,1024]{1,0:T(8,128)S(1)} collective-permute-done((f32[128,1024]{1,0:T(8,128)}, f32[128,1024]{1,0:T(8,128)S(1)}, u32[]{:S(2)}, u32[]{:S(2)}) %collective-permute-start.1) | collective-permute-done | bytes 524320 | tf_op jit(solution)/shard_map/ppermute | solution.py:72
  60.4 0.0 collective-permute-done.2
  60.5 1.2 %maximum_bitcast_fusion = f32[16,8,8,128]{3,1,2,0:T(8,128)S(1)} fusion(f32[128,1024]{1,0:T(8,128)} %maxima.7, f32[128,1024]{1,0:T(8,128)S(1)} %collective-permute-done.2, f32[128,1024]{1,0:T(8,128)S(1)} %collective-permute-done, f32[128,1024]{1,0:T(8,128)S(1)} %collective-permute-done.1), kind=kLoop, calls=%fused_computation.2 | loop fusion | flops 393216 | bytes 2621440
  61.6 0.1 copy.8
  61.7 0.2 fusion
  61.9 1.6 %collective-permute-start.3 = (f32[128,128]{1,0:T(8,128)S(1)}, f32[128,128]{1,0:T(8,128)S(1)}, u32[]{:S(2)}, u32[]{:S(2)}) collective-permute-start(f32[128,128]{1,0:T(8,128)S(1)} %fusion), channel_id=1, source_target_pairs={{0,4},{4,0},{8,12},{12,8},{1,5},{5,1},{9,13},{13,9},{2,6},{6,2},{1... | collective-permute-start | bytes 196616 | tf_op jit(solution)/shard_map/ppermute | solution.py:72
  63.5 2.8 %collective-permute-done.3 = f32[128,128]{1,0:T(8,128)S(1)} collective-permute-done((f32[128,128]{1,0:T(8,128)S(1)}, f32[128,128]{1,0:T(8,128)S(1)}, u32[]{:S(2)}, u32[]{:S(2)}) %collective-permute-start.3) | collective-permute-done | bytes 65568 | tf_op jit(solution)/shard_map/ppermute | solution.py:72
  66.3 1.6 %collective-permute-start.4 = (f32[128,128]{1,0:T(8,128)S(1)}, f32[128,128]{1,0:T(8,128)S(1)}, u32[]{:S(2)}, u32[]{:S(2)}) collective-permute-start(f32[128,128]{1,0:T(8,128)S(1)} %add.37), channel_id=1, source_target_pairs={{0,8},{4,12},{8,0},{12,4},{1,9},{5,13},{9,1},{13,5},{2,10},{6,14},... | collective-permute-start | bytes 196616 | tf_op jit(solution)/shard_map/ppermute | solution.py:72
  67.8 2.7 %collective-permute-done.4 = f32[128,128]{1,0:T(8,128)S(1)} collective-permute-done((f32[128,128]{1,0:T(8,128)S(1)}, f32[128,128]{1,0:T(8,128)S(1)}, u32[]{:S(2)}, u32[]{:S(2)}) %collective-permute-start.4) | collective-permute-done | bytes 65568 | tf_op jit(solution)/shard_map/ppermute | solution.py:72
  70.7 0.1 collective-permute-start.5
  70.7 1.1 %collective-permute-done.5 = f32[2,128]{1,0:T(2,128)S(1)} collective-permute-done((f32[2,128]{1,0:T(2,128)S(1)}, f32[2,128]{1,0:T(2,128)S(1)}, u32[]{:S(2)}, u32[]{:S(2)}) %collective-permute-start.5) | collective-permute-done | bytes 1056 | tf_op jit(solution)/shard_map/ppermute | solution.py:72
  71.9 0.1 collective-permute-start.6
  72.0 3.6 %collective-permute-done.6 = f32[2,128]{1,0:T(2,128)S(1)} collective-permute-done((f32[2,128]{1,0:T(2,128)S(1)}, f32[2,128]{1,0:T(2,128)S(1)}, u32[]{:S(2)}, u32[]{:S(2)}) %collective-permute-start.6) | collective-permute-done | bytes 1056 | tf_op jit(solution)/shard_map/ppermute | solution.py:72
  75.6 1.1 %collective-permute-start.7 = (f32[2,128]{1,0:T(2,128)S(1)}, f32[2,128]{1,0:T(2,128)S(1)}, u32[]{:S(2)}, u32[]{:S(2)}) collective-permute-start(f32[2,128]{1,0:T(2,128)S(1)} %pad_maximum_fusion.2), channel_id=1, source_target_pairs={{0,2},{1,3},{2,0},{3,1},{4,6},{5,7},{6,4},{7,5},{8,10},{9,11},{10,... | collective-permute-start | bytes 3080 | tf_op jit(solution)/shard_map/ppermute | solution.py:72
  76.7 3.5 %collective-permute-done.7 = f32[2,128]{1,0:T(2,128)S(1)} collective-permute-done((f32[2,128]{1,0:T(2,128)S(1)}, f32[2,128]{1,0:T(2,128)S(1)}, u32[]{:S(2)}, u32[]{:S(2)}) %collective-permute-start.7) | collective-permute-done | bytes 1056 | tf_op jit(solution)/shard_map/ppermute | solution.py:72
  80.2 0.7 copy.7
  (11 shorter events, 0.2 us)
Async XLA Ops:
  10.4 28.0 %collective-permute-start = (f32[128,1024]{1,0:T(8,128)}, f32[128,1024]{1,0:T(8,128)S(1)}, u32[]{:S(2)}, u32[]{:S(2)}) collective-permute-start(f32[128,1024]{1,0:T(8,128)} %maxima.4), channel_id=1, source_target_pairs={{0,3},{1,2},{2,1},{3,0},{4,7},{5,6},{6,5},{7,4},{8,11},{9,10},{10,... | collective-permute-start | bytes 1572872 | tf_op jit(solution)/shard_map/ppermute | solution.py:72
  22.9 8.0 %copy-start = (s32[128]{0:T(128)S(1)}, s32[128]{0:T(128)}, u32[]{:S(2)}) copy-start(s32[128]{0:T(128)} %param.7) | copy-start | bytes 1540
  22.9 37.6 %collective-permute-start.1 = (f32[128,1024]{1,0:T(8,128)}, f32[128,1024]{1,0:T(8,128)S(1)}, u32[]{:S(2)}, u32[]{:S(2)}) collective-permute-start(f32[128,1024]{1,0:T(8,128)} %maxima.5), channel_id=1, source_target_pairs={{0,2},{1,3},{2,0},{3,1},{4,6},{5,7},{6,4},{7,5},{8,10},{9,11},{10,... | collective-permute-start | bytes 1572872 | tf_op jit(solution)/shard_map/ppermute | solution.py:72
  30.5 30.0 %collective-permute-start.2 = (f32[128,1024]{1,0:T(8,128)}, f32[128,1024]{1,0:T(8,128)S(1)}, u32[]{:S(2)}, u32[]{:S(2)}) collective-permute-start(f32[128,1024]{1,0:T(8,128)} %maxima.6), channel_id=1, source_target_pairs={{0,1},{1,0},{2,3},{3,2},{4,5},{5,4},{6,7},{7,6},{8,9},{9,8},{10,11... | collective-permute-start | bytes 1572872 | tf_op jit(solution)/shard_map/ppermute | solution.py:72
  61.9 4.3 %collective-permute-start.3 = (f32[128,128]{1,0:T(8,128)S(1)}, f32[128,128]{1,0:T(8,128)S(1)}, u32[]{:S(2)}, u32[]{:S(2)}) collective-permute-start(f32[128,128]{1,0:T(8,128)S(1)} %fusion), channel_id=1, source_target_pairs={{0,4},{4,0},{8,12},{12,8},{1,5},{5,1},{9,13},{13,9},{2,6},{6,2},{1... | collective-permute-start | bytes 196616 | tf_op jit(solution)/shard_map/ppermute | solution.py:72
  66.3 4.3 %collective-permute-start.4 = (f32[128,128]{1,0:T(8,128)S(1)}, f32[128,128]{1,0:T(8,128)S(1)}, u32[]{:S(2)}, u32[]{:S(2)}) collective-permute-start(f32[128,128]{1,0:T(8,128)S(1)} %add.37), channel_id=1, source_target_pairs={{0,8},{4,12},{8,0},{12,4},{1,9},{5,13},{9,1},{13,5},{2,10},{6,14},... | collective-permute-start | bytes 196616 | tf_op jit(solution)/shard_map/ppermute | solution.py:72
  70.7 1.2 %collective-permute-start.5 = (f32[2,128]{1,0:T(2,128)S(1)}, f32[2,128]{1,0:T(2,128)S(1)}, u32[]{:S(2)}, u32[]{:S(2)}) collective-permute-start(f32[2,128]{1,0:T(2,128)S(1)} %pad_maximum_fusion), channel_id=1, source_target_pairs={{0,16},{16,0},{1,17},{17,1},{2,18},{18,2},{3,19},{19,3},{4,20},{20... | collective-permute-start | bytes 3080 | tf_op jit(solution)/shard_map/ppermute | solution.py:72
  71.9 3.6 %collective-permute-start.6 = (f32[2,128]{1,0:T(2,128)S(1)}, f32[2,128]{1,0:T(2,128)S(1)}, u32[]{:S(2)}, u32[]{:S(2)}) collective-permute-start(f32[2,128]{1,0:T(2,128)S(1)} %pad_maximum_fusion.1), channel_id=1, source_target_pairs={{0,1},{1,0},{2,3},{3,2},{4,5},{5,4},{6,7},{7,6},{8,9},{9,8},{10,11... | collective-permute-start | bytes 3080 | tf_op jit(solution)/shard_map/ppermute | solution.py:72
  75.6 4.5 %collective-permute-start.7 = (f32[2,128]{1,0:T(2,128)S(1)}, f32[2,128]{1,0:T(2,128)S(1)}, u32[]{:S(2)}, u32[]{:S(2)}) collective-permute-start(f32[2,128]{1,0:T(2,128)S(1)} %pad_maximum_fusion.2), channel_id=1, source_target_pairs={{0,2},{1,3},{2,0},{3,1},{4,6},{5,7},{6,4},{7,5},{8,10},{9,11},{10,... | collective-permute-start | bytes 3080 | tf_op jit(solution)/shard_map/ppermute | solution.py:72

commit v2 on v1

v2 whole, which is shorter than its diff:
```python
import functools

import jax
import jax.numpy as jnp
from jax import lax
from jax.experimental import pallas as pl
from jax.experimental.pallas import tpu as pltpu
from jax.sharding import PartitionSpec as P

masked_low = -1e30
mebibyte = 2**20


def maxima_kernel(len_ref, queries_ref, passages_ref, out_ref, *, distance, block_size, offset, rows, columns):
    _, token_count, width = passages_ref.shape
    passage_count, query_rows = out_ref.shape
    per_dot = rows // token_count
    gz = lax.axis_index("gz")
    first = (gz ^ distance) * block_size + offset
    hidden = gz * token_count
    token_ids = lax.broadcasted_iota(jnp.int32, (token_count, columns), 0)
    for m in range(passage_count // per_dot):
        tile = passages_ref[pl.ds(first + m * per_dot, per_dot)].reshape(rows, width)
        for j in range(query_rows // columns):
            scores = lax.dot_general(
                tile,
                queries_ref[j * columns : (j + 1) * columns],
                (((1,), (1,)), ((), ())),
                preferred_element_type=jnp.float32,
            )
            best = []
            for k in range(per_dot):
                usable = token_ids < len_ref[first + m * per_dot + k] - hidden
                mine = jnp.where(usable, scores[k * token_count : (k + 1) * token_count], masked_low)
                best.append(jnp.max(mine, axis=0, keepdims=True))
            out_ref[m * per_dot : (m + 1) * per_dot, j * columns : (j + 1) * columns] = (
                jnp.concatenate(best, axis=0)
            )


def maxima(flat_queries, passages, passage_len, distance, block_size, offset, size):
    _, token_count, width = passages.shape
    query_rows = flat_queries.shape[0]
    per_dot = min(size, max(1, 1024 // token_count))
    return pl.pallas_call(
        functools.partial(
            maxima_kernel,
            distance=distance,
            block_size=block_size,
            offset=offset,
            rows=per_dot * token_count,
            columns=min(256, query_rows),
        ),
        in_specs=[
            pl.BlockSpec(memory_space=pltpu.SMEM),
            pl.BlockSpec(memory_space=pltpu.VMEM),
            pl.BlockSpec(memory_space=pltpu.VMEM),
        ],
        out_specs=pl.BlockSpec(memory_space=pltpu.VMEM),
        out_shape=jax.ShapeDtypeStruct((size, query_rows), jnp.float32),
        cost_estimate=pl.CostEstimate(
            flops=2 * 2 * size * token_count * query_rows * width,
            bytes_accessed=size * (token_count * width * 2 + query_rows * 4),
            transcendentals=0,
        ),
        compiler_params=pltpu.CompilerParams(vmem_limit_bytes=12 * mebibyte),
        name=f"maxima_{distance}_{offset}",
    )(passage_len, flat_queries, passages)


def merge_kernel(*refs):
    *part_refs, len_ref, out_ref = refs
    query_count = out_ref.shape[1]
    lanes = part_refs[0].shape[1]
    query_rows = lanes // query_count
    merged = functools.reduce(jnp.maximum, [part[...] for part in part_refs])
    shape = (lanes, query_count)
    row = lax.broadcasted_iota(jnp.int32, shape, 0)
    start = lax.broadcasted_iota(jnp.int32, shape, 1) * query_rows
    used = jnp.clip(len_ref[...] - lax.axis_index("gy") * query_rows, 0, query_rows)
    counted = jnp.where((row >= start) & (row < start + used), 1.0, 0.0).astype(jnp.bfloat16)
    total = None
    for _ in range(3):
        piece = merged.astype(jnp.bfloat16)
        merged = merged - piece.astype(jnp.float32)
        term = jnp.dot(piece, counted, preferred_element_type=jnp.float32)
        total = term if total is None else total + term
    out_ref[...] = total


def merge(parts, query_len):
    query_count = query_len.shape[0]
    block_size = parts[0].shape[0]
    return pl.pallas_call(
        merge_kernel,
        out_shape=jax.ShapeDtypeStruct((block_size, query_count), jnp.float32),
        compiler_params=pltpu.CompilerParams(vmem_limit_bytes=12 * mebibyte),
        name="merge",
    )(*parts, query_len.reshape(1, query_count))


def exchange(array, axis, distance):
    size = lax.axis_size(axis)
    return lax.ppermute(array, axis, [(k, k ^ distance) for k in range(size)])


def hypercube(array, axis, combine):
    distance = 1
    while distance < lax.axis_size(axis):
        array = combine(array, exchange(array, axis, distance))
        distance *= 2
    return array


def join_pairs(one, other):
    top = jnp.maximum(one[0], other[0])
    summed = one[1] * jnp.exp(one[0] - top) + other[1] * jnp.exp(other[0] - top)
    return jnp.stack([top, summed])


def owned_maxima(score, block_size, owners):
    if owners != 4:
        return [
            exchange(score(distance, 0, block_size), "gz", distance) if distance else score(0, 0, block_size)
            for distance in range(owners - 1, -1, -1)
        ]
    half = block_size // 2
    near = [exchange(score(3, part * half, half), "gz", 1) for part in range(2)]
    far = []
    for part in range(2):
        joined = jnp.maximum(score(2, part * half, half), near[part])
        far.append(exchange(joined, "gz", 2))
    beside = exchange(score(1, 0, block_size), "gz", 1)
    return [score(0, 0, block_size), beside, jnp.concatenate(far)]


def shards(queries, passages, passage_len, query_len):
    query_count, query_rows, width = queries.shape
    passage_count = passages.shape[0]
    owners = lax.axis_size("gz")
    block_size = passage_count // owners
    flat_queries = queries.reshape(query_count * query_rows, width)
    held = pltpu.with_memory_space_constraint(passages, pltpu.VMEM)

    def score(distance, offset, size):
        return maxima(flat_queries, held, passage_len, distance, block_size, offset, size)

    partial_value = merge(owned_maxima(score, block_size, owners), query_len)
    scores = hypercube(partial_value, "gy", jnp.add)
    top = jnp.max(scores, axis=0)
    summed = jnp.sum(jnp.exp(scores - top[None]), axis=0)
    pair = hypercube(jnp.stack([top, summed]), "gx", join_pairs)
    pair = hypercube(pair, "gz", join_pairs)
    return jnp.transpose(scores - (pair[0] + jnp.log(pair[1]))[None])


def solution(mesh):
    return jax.shard_map(
        shards,
        mesh=mesh,
        in_specs=(P(None, "gy", None), P("gx", "gz", None), P("gx"), P()),
        out_specs=P(None, ("gx", "gz")),
        check_vma=False,
    )
```

time: 81.3 us -> 72 us (0.89)
  Pallas kernels: 29.8 us -> 22.4 us
  waiting for transfers between devices: 35.7 us -> 30.5 us
  local copies, waits for them, and re-layouts: 2.54 us -> 5.75 us
  starting transfers between devices: 9.88 us -> 12.7 us
  other arithmetic: 2.84 us -> 0.26 us
    pallas_call x4 -> x7, Pallas kernels: 29.8 us -> 22.4 us  [the longest x6 21.9 us: maxima(): pl.pallas_call(functools.partial(maxima_kernel, distance=distance, block_...]
    ppermute x8 -> x10, waiting for transfers between devices: 35.7 us -> 30.5 us  [exchange(): return lax.ppermute(array, axis, [(k, k ^ distance) for k in range(size)])]
    unnamed x3 -> x8, local copies, waits for them, and re-layouts: 0.1 us -> 5.02 us
    ppermute x8 -> x10, starting transfers between devices: 9.88 us -> 12.7 us  [exchange(): return lax.ppermute(array, axis, [(k, k ^ distance) for k in range(size)])]
    transpose x1 -> x0, local copies, waits for them, and re-layouts: 1.7 us -> none  [shards(): jnp.transpose(queries, (1, 0, 2)).reshape(query_rows * query_count, width)]
    sub x1 -> x0, other arithmetic: 1.26 us -> none  [shards(): usable_tokens = passage_len - gz * token_count]
    unnamed x1 -> x0, other arithmetic: 1.19 us -> none
  transfers between devices with their start and end apart: 8 -> 10, of which waited for: 6 -> 7; matrix products, arithmetic and copies ran while one was open for 0% -> 0% of each run, Pallas kernels for 28% -> 26%
where the time goes in v2:
time: 72 us; the launch traced here: 71.8 us
  waiting for transfers between devices  30.5 us (42%)
  Pallas kernels  22.4 us (31%)
  starting transfers between devices  12.7 us (18%)
  local copies, waits for them, and re-layouts  5.75 us (8%)
    ppermute x10, waiting for transfers between devices, exchange(): return lax.ppermute(array, axis, [(k, k ^ distance) for k in range(size)])  30.5 us
    pallas_call x6, Pallas kernels, maxima(): pl.pallas_call(functools.partial(maxima_kernel, distance=distance, block_...  21.9 us
    ppermute x10, starting transfers between devices, exchange(): return lax.ppermute(array, axis, [(k, k ^ distance) for k in range(size)])  12.7 us
    unnamed x8, local copies, waits for them, and re-layouts  5.02 us
  transfers between devices with their start and end apart: 10, of which 7 were waited for; matrix products, arithmetic and copies ran while one was open for 0% of the time, Pallas kernels for 26%

profile of v2, /device:TPU:0, one launch (start us, length us, event | category | flops | bytes accessed | tf_op | source)
XLA Modules:
  0.0 71.8 jit_solution(3308595953503811196)
XLA Ops:
  0.0 0.0 copy-start
  0.0 3.4 %copy-done = bf16[512,64,128]{2,1,0:T(8,128)(2,1)S(1)} copy-done((bf16[512,64,128]{2,1,0:T(8,128)(2,1)S(1)}, bf16[512,64,128]{2,1,0:T(8,128)(2,1)}, u32[]{:S(2)}) %copy-start) | copy-done | bytes 8388632
  3.4 0.0 copy-start.1
  3.4 0.9 %copy-done.1 = bf16[128,8,128]{2,1,0:T(8,128)(2,1)S(1)} copy-done((bf16[128,8,128]{2,1,0:T(8,128)(2,1)S(1)}, bf16[128,8,128]{2,1,0:T(8,128)(2,1)}, u32[]{:S(2)}) %copy-start.1) | copy-done | bytes 262168
  4.3 0.0 copy-start.2
  4.3 0.7 copy-done.2
  5.0 2.9 %maxima_3_0.1 = f32[64,1024]{1,0:T(8,128)S(1)} custom-call(s32[512]{0:T(512)S(1)} %copy-done.2, bf16[1024,128]{1,0:T(8,128)(2,1)S(1)} %bitcast.12, bf16[512,64,128]{2,1,0:T(8,128)(2,1)S(1)} %copy-done), custom_call_target="tpu_custom_call" | custom-call | flops 2147483648 | bytes 1310720 | tf_op jit(solution)/shard_map/maxima_3_0/pallas_call | solution.py:45
  7.9 3.1 %collective-permute-start.1 = (f32[64,1024]{1,0:T(8,128)S(1)}, f32[64,1024]{1,0:T(8,128)S(1)}, u32[]{:S(2)}, u32[]{:S(2)}) collective-permute-start(f32[64,1024]{1,0:T(8,128)S(1)} %maxima_3_0.1), channel_id=1, source_target_pairs={{0,1},{1,0},{2,3},{3,2},{4,5},{5,4},{6,7},{7,6},{8,9},{9,8},{10,11... | collective-permute-start | bytes 786440 | tf_op jit(solution)/shard_map/ppermute | solution.py:104
  11.1 2.9 %maxima_3_64.1 = f32[64,1024]{1,0:T(8,128)S(1)} custom-call(s32[512]{0:T(512)S(1)} %copy-done.2, bf16[1024,128]{1,0:T(8,128)(2,1)S(1)} %bitcast.13, bf16[512,64,128]{2,1,0:T(8,128)(2,1)S(1)} %copy-done), custom_call_target="tpu_custom_call" | custom-call | flops 2147483648 | bytes 1310720 | tf_op jit(solution)/shard_map/maxima_3_64/pallas_call | solution.py:45
  14.0 0.1 collective-permute-start.3
  14.1 5.1 %maxima_1_0.1 = f32[128,1024]{1,0:T(8,128)S(1)} custom-call(s32[512]{0:T(512)S(1)} %copy-done.2, bf16[1024,128]{1,0:T(8,128)(2,1)S(1)} %bitcast.14, bf16[512,64,128]{2,1,0:T(8,128)(2,1)S(1)} %copy-done), custom_call_target="tpu_custom_call" | custom-call | flops 4294967296 | bytes 2621440 | tf_op jit(solution)/shard_map/maxima_1_0/pallas_call | solution.py:45
  19.2 2.1 %collective-permute-start = (f32[128,1024]{1,0:T(8,128)S(1)}, f32[128,1024]{1,0:T(8,128)S(1)}, u32[]{:S(2)}, u32[]{:S(2)}) collective-permute-start(f32[128,1024]{1,0:T(8,128)S(1)} %maxima_1_0.1), channel_id=1, source_target_pairs={{0,1},{1,0},{2,3},{3,2},{4,5},{5,4},{6,7},{7,6},{8,9},{9,8},{10,11... | collective-permute-start | bytes 1572872 | tf_op jit(solution)/shard_map/ppermute | solution.py:104
  21.3 2.9 %maxima_2_0.1 = f32[64,1024]{1,0:T(8,128)S(1)} custom-call(s32[512]{0:T(512)S(1)} %copy-done.2, bf16[1024,128]{1,0:T(8,128)(2,1)S(1)} %bitcast.15, bf16[512,64,128]{2,1,0:T(8,128)(2,1)S(1)} %copy-done), custom_call_target="tpu_custom_call" | custom-call | flops 2147483648 | bytes 1310720 | tf_op jit(solution)/shard_map/maxima_2_0/pallas_call | solution.py:45
  24.2 2.9 %maxima_2_64.1 = f32[64,1024]{1,0:T(8,128)S(1)} custom-call(s32[512]{0:T(512)S(1)} %copy-done.2, bf16[1024,128]{1,0:T(8,128)(2,1)S(1)} %bitcast.16, bf16[512,64,128]{2,1,0:T(8,128)(2,1)S(1)} %copy-done), custom_call_target="tpu_custom_call" | custom-call | flops 2147483648 | bytes 1310720 | tf_op jit(solution)/shard_map/maxima_2_64/pallas_call | solution.py:45
  27.1 0.0 collective-permute-done.1
  27.2 2.7 %collective-permute-start.2 = (f32[64,1024]{1,0:T(8,128)S(1)}, f32[64,1024]{1,0:T(8,128)S(1)}, u32[]{:S(2)}, u32[]{:S(2)}) collective-permute-start(f32[64,1024]{1,0:T(8,128)S(1)} %max.24), channel_id=1, source_target_pairs={{0,2},{1,3},{2,0},{3,1},{4,6},{5,7},{6,4},{7,5},{8,10},{9,11},{10,... | collective-permute-start | bytes 786440 | tf_op jit(solution)/shard_map/ppermute | solution.py:104
  29.8 0.0 collective-permute-done.3
  29.8 0.0 copy-start.3
  29.9 0.4 collective-permute-start.4
  30.3 5.1 %maxima_0_0.1.refs_0_ = f32[128,1024]{1,0:T(8,128)S(1)} custom-call(s32[512]{0:T(512)S(1)} %copy-done.2, bf16[1024,128]{1,0:T(8,128)(2,1)S(1)} %bitcast.17, bf16[512,64,128]{2,1,0:T(8,128)(2,1)S(1)} %copy-done), custom_call_target="tpu_custom_call" | custom-call | flops 4294967296 | bytes 2621440 | tf_op jit(solution)/shard_map/maxima_0_0/pallas_call | solution.py:45
  35.4 13.2 %collective-permute-done.2 = f32[64,1024]{1,0:T(8,128)S(1)} collective-permute-done((f32[64,1024]{1,0:T(8,128)S(1)}, f32[64,1024]{1,0:T(8,128)S(1)}, u32[]{:S(2)}, u32[]{:S(2)}) %collective-permute-start.2) | collective-permute-done | bytes 262176 | tf_op jit(solution)/shard_map/ppermute | solution.py:104
  48.5 3.7 %collective-permute-done.4 = f32[64,1024]{1,0:T(8,128)S(1)} collective-permute-done((f32[64,1024]{1,0:T(8,128)S(1)}, f32[64,1024]{1,0:T(8,128)S(1)}, u32[]{:S(2)}, u32[]{:S(2)}) %collective-permute-start.4) | collective-permute-done | bytes 262176 | tf_op jit(solution)/shard_map/ppermute | solution.py:104
  52.3 0.0 collective-permute-done.refs_1_
  52.3 0.0 copy-done.3
  52.3 0.5 merge.1
  52.8 1.6 %collective-permute-start.5 = (f32[128,128]{1,0:T(8,128)S(1)}, f32[128,128]{1,0:T(8,128)S(1)}, u32[]{:S(2)}, u32[]{:S(2)}) collective-permute-start(f32[128,128]{1,0:T(8,128)S(1)} %merge.1), channel_id=1, source_target_pairs={{0,4},{4,0},{8,12},{12,8},{1,5},{5,1},{9,13},{13,9},{2,6},{6,2},{1... | collective-permute-start | bytes 196616 | tf_op jit(solution)/shard_map/ppermute | solution.py:104
  54.4 2.8 %collective-permute-done.5 = f32[128,128]{1,0:T(8,128)S(1)} collective-permute-done((f32[128,128]{1,0:T(8,128)S(1)}, f32[128,128]{1,0:T(8,128)S(1)}, u32[]{:S(2)}, u32[]{:S(2)}) %collective-permute-start.5) | collective-permute-done | bytes 65568 | tf_op jit(solution)/shard_map/ppermute | solution.py:104
  57.1 1.6 %collective-permute-start.6 = (f32[128,128]{1,0:T(8,128)S(1)}, f32[128,128]{1,0:T(8,128)S(1)}, u32[]{:S(2)}, u32[]{:S(2)}) collective-permute-start(f32[128,128]{1,0:T(8,128)S(1)} %add.25), channel_id=1, source_target_pairs={{0,8},{4,12},{8,0},{12,4},{1,9},{5,13},{9,1},{13,5},{2,10},{6,14},... | collective-permute-start | bytes 196616 | tf_op jit(solution)/shard_map/ppermute | solution.py:104
  58.7 2.7 %collective-permute-done.6 = f32[128,128]{1,0:T(8,128)S(1)} collective-permute-done((f32[128,128]{1,0:T(8,128)S(1)}, f32[128,128]{1,0:T(8,128)S(1)}, u32[]{:S(2)}, u32[]{:S(2)}) %collective-permute-start.6) | collective-permute-done | bytes 65568 | tf_op jit(solution)/shard_map/ppermute | solution.py:104
  61.6 0.1 collective-permute-start.7
  61.6 1.1 %collective-permute-done.7 = f32[2,128]{1,0:T(2,128)S(1)} collective-permute-done((f32[2,128]{1,0:T(2,128)S(1)}, f32[2,128]{1,0:T(2,128)S(1)}, u32[]{:S(2)}, u32[]{:S(2)}) %collective-permute-start.7) | collective-permute-done | bytes 1056 | tf_op jit(solution)/shard_map/ppermute | solution.py:104
  62.8 0.1 collective-permute-start.8
  62.9 3.6 %collective-permute-done.8 = f32[2,128]{1,0:T(2,128)S(1)} collective-permute-done((f32[2,128]{1,0:T(2,128)S(1)}, f32[2,128]{1,0:T(2,128)S(1)}, u32[]{:S(2)}, u32[]{:S(2)}) %collective-permute-start.8) | collective-permute-done | bytes 1056 | tf_op jit(solution)/shard_map/ppermute | solution.py:104
  66.5 1.1 %collective-permute-start.9 = (f32[2,128]{1,0:T(2,128)S(1)}, f32[2,128]{1,0:T(2,128)S(1)}, u32[]{:S(2)}, u32[]{:S(2)}) collective-permute-start(f32[2,128]{1,0:T(2,128)S(1)} %pad_maximum_fusion.3), channel_id=1, source_target_pairs={{0,2},{1,3},{2,0},{3,1},{4,6},{5,7},{6,4},{7,5},{8,10},{9,11},{10,... | collective-permute-start | bytes 3080 | tf_op jit(solution)/shard_map/ppermute | solution.py:104
  67.6 3.5 %collective-permute-done.9 = f32[2,128]{1,0:T(2,128)S(1)} collective-permute-done((f32[2,128]{1,0:T(2,128)S(1)}, f32[2,128]{1,0:T(2,128)S(1)}, u32[]{:S(2)}, u32[]{:S(2)}) %collective-permute-start.9) | collective-permute-done | bytes 1056 | tf_op jit(solution)/shard_map/ppermute | solution.py:104
  71.0 0.7 %copy.5 = f32[128,128]{1,0:T(8,128)} copy(f32[128,128]{0,1:T(8,128)S(1)} %subtract_bitcast_fusion) | data formatting | bytes 131072 | tf_op jit(solution)/shard_map/transpose | solution.py:154
  (13 shorter events, 0.3 us)
Async XLA Ops:
  0.0 3.4 %copy-start = (bf16[512,64,128]{2,1,0:T(8,128)(2,1)S(1)}, bf16[512,64,128]{2,1,0:T(8,128)(2,1)}, u32[]{:S(2)}) copy-start(bf16[512,64,128]{2,1,0:T(8,128)(2,1)} %passages_ref.11) | copy-start | bytes 25165828
  3.4 0.9 %copy-start.1 = (bf16[128,8,128]{2,1,0:T(8,128)(2,1)S(1)}, bf16[128,8,128]{2,1,0:T(8,128)(2,1)}, u32[]{:S(2)}) copy-start(bf16[128,8,128]{2,1,0:T(8,128)(2,1)} %param.4) | copy-start | bytes 786436
  4.3 0.7 copy-start.2
  7.9 19.2 %collective-permute-start.1 = (f32[64,1024]{1,0:T(8,128)S(1)}, f32[64,1024]{1,0:T(8,128)S(1)}, u32[]{:S(2)}, u32[]{:S(2)}) collective-permute-start(f32[64,1024]{1,0:T(8,128)S(1)} %maxima_3_0.1), channel_id=1, source_target_pairs={{0,1},{1,0},{2,3},{3,2},{4,5},{5,4},{6,7},{7,6},{8,9},{9,8},{10,11... | collective-permute-start | bytes 786440 | tf_op jit(solution)/shard_map/ppermute | solution.py:104
  14.0 15.8 %collective-permute-start.3 = (f32[64,1024]{1,0:T(8,128)S(1)}, f32[64,1024]{1,0:T(8,128)S(1)}, u32[]{:S(2)}, u32[]{:S(2)}) collective-permute-start(f32[64,1024]{1,0:T(8,128)S(1)} %maxima_3_64.1), channel_id=1, source_target_pairs={{0,1},{1,0},{2,3},{3,2},{4,5},{5,4},{6,7},{7,6},{8,9},{9,8},{10,11... | collective-permute-start | bytes 786440 | tf_op jit(solution)/shard_map/ppermute | solution.py:104
  19.2 33.1 %collective-permute-start = (f32[128,1024]{1,0:T(8,128)S(1)}, f32[128,1024]{1,0:T(8,128)S(1)}, u32[]{:S(2)}, u32[]{:S(2)}) collective-permute-start(f32[128,1024]{1,0:T(8,128)S(1)} %maxima_1_0.1), channel_id=1, source_target_pairs={{0,1},{1,0},{2,3},{3,2},{4,5},{5,4},{6,7},{7,6},{8,9},{9,8},{10,11... | collective-permute-start | bytes 1572872 | tf_op jit(solution)/shard_map/ppermute | solution.py:104
  27.2 21.4 %collective-permute-start.2 = (f32[64,1024]{1,0:T(8,128)S(1)}, f32[64,1024]{1,0:T(8,128)S(1)}, u32[]{:S(2)}, u32[]{:S(2)}) collective-permute-start(f32[64,1024]{1,0:T(8,128)S(1)} %max.24), channel_id=1, source_target_pairs={{0,2},{1,3},{2,0},{3,1},{4,6},{5,7},{6,4},{7,5},{8,10},{9,11},{10,... | collective-permute-start | bytes 786440 | tf_op jit(solution)/shard_map/ppermute | solution.py:104
  29.8 22.4 %copy-start.3 = (s32[128]{0:T(128)S(1)}, s32[128]{0:T(128)}, u32[]{:S(2)}) copy-start(s32[128]{0:T(128)} %param.7) | copy-start | bytes 1540
  29.9 22.4 %collective-permute-start.4 = (f32[64,1024]{1,0:T(8,128)S(1)}, f32[64,1024]{1,0:T(8,128)S(1)}, u32[]{:S(2)}, u32[]{:S(2)}) collective-permute-start(f32[64,1024]{1,0:T(8,128)S(1)} %max.25), channel_id=1, source_target_pairs={{0,2},{1,3},{2,0},{3,1},{4,6},{5,7},{6,4},{7,5},{8,10},{9,11},{10,... | collective-permute-start | bytes 786440 | tf_op jit(solution)/shard_map/ppermute | solution.py:104
  52.8 4.3 %collective-permute-start.5 = (f32[128,128]{1,0:T(8,128)S(1)}, f32[128,128]{1,0:T(8,128)S(1)}, u32[]{:S(2)}, u32[]{:S(2)}) collective-permute-start(f32[128,128]{1,0:T(8,128)S(1)} %merge.1), channel_id=1, source_target_pairs={{0,4},{4,0},{8,12},{12,8},{1,5},{5,1},{9,13},{13,9},{2,6},{6,2},{1... | collective-permute-start | bytes 196616 | tf_op jit(solution)/shard_map/ppermute | solution.py:104
  57.1 4.3 %collective-permute-start.6 = (f32[128,128]{1,0:T(8,128)S(1)}, f32[128,128]{1,0:T(8,128)S(1)}, u32[]{:S(2)}, u32[]{:S(2)}) collective-permute-start(f32[128,128]{1,0:T(8,128)S(1)} %add.25), channel_id=1, source_target_pairs={{0,8},{4,12},{8,0},{12,4},{1,9},{5,13},{9,1},{13,5},{2,10},{6,14},... | collective-permute-start | bytes 196616 | tf_op jit(solution)/shard_map/ppermute | solution.py:104
  61.6 1.2 %collective-permute-start.7 = (f32[2,128]{1,0:T(2,128)S(1)}, f32[2,128]{1,0:T(2,128)S(1)}, u32[]{:S(2)}, u32[]{:S(2)}) collective-permute-start(f32[2,128]{1,0:T(2,128)S(1)} %pad_maximum_fusion.1), channel_id=1, source_target_pairs={{0,16},{16,0},{1,17},{17,1},{2,18},{18,2},{3,19},{19,3},{4,20},{20... | collective-permute-start | bytes 3080 | tf_op jit(solution)/shard_map/ppermute | solution.py:104
  62.8 3.6 %collective-permute-start.8 = (f32[2,128]{1,0:T(2,128)S(1)}, f32[2,128]{1,0:T(2,128)S(1)}, u32[]{:S(2)}, u32[]{:S(2)}) collective-permute-start(f32[2,128]{1,0:T(2,128)S(1)} %pad_maximum_fusion.2), channel_id=1, source_target_pairs={{0,1},{1,0},{2,3},{3,2},{4,5},{5,4},{6,7},{7,6},{8,9},{9,8},{10,11... | collective-permute-start | bytes 3080 | tf_op jit(solution)/shard_map/ppermute | solution.py:104
  66.5 4.5 %collective-permute-start.9 = (f32[2,128]{1,0:T(2,128)S(1)}, f32[2,128]{1,0:T(2,128)S(1)}, u32[]{:S(2)}, u32[]{:S(2)}) collective-permute-start(f32[2,128]{1,0:T(2,128)S(1)} %pad_maximum_fusion.3), channel_id=1, source_target_pairs={{0,2},{1,3},{2,0},{3,1},{4,6},{5,7},{6,4},{7,5},{8,10},{9,11},{10,... | collective-permute-start | bytes 3080 | tf_op jit(solution)/shard_map/ppermute | solution.py:104

commit v3 on v2

v3 whole, which is shorter than its diff:
```python
import functools

import jax
import jax.numpy as jnp
from jax import lax
from jax.experimental import pallas as pl
from jax.experimental.pallas import tpu as pltpu
from jax.sharding import PartitionSpec as P


masked_low = -1e30
mebibyte = 2**20


def best_tokens(len_ref, queries_ref, passages_ref, out_ref, first, place, rows, columns):
    _, token_count, width = passages_ref.shape
    query_rows = out_ref.shape[1]
    per_dot = rows // token_count
    hidden = lax.axis_index("gz") * token_count
    token_ids = lax.broadcasted_iota(jnp.int32, (token_count, columns), 0)
    tile = passages_ref[pl.ds(first, per_dot)].reshape(rows, width)
    for j in range(query_rows // columns):
        scores = lax.dot_general(
            tile,
            queries_ref[j * columns : (j + 1) * columns],
            (((1,), (1,)), ((), ())),
            preferred_element_type=jnp.float32,
        )
        best = []
        for k in range(per_dot):
            usable = token_ids < len_ref[first + k] - hidden
            mine = jnp.where(usable, scores[k * token_count : (k + 1) * token_count], masked_low)
            best.append(jnp.max(mine, axis=0, keepdims=True))
        out_ref[place : place + per_dot, j * columns : (j + 1) * columns] = jnp.concatenate(best, axis=0)


def first_kernel(
    len_hbm, queries_hbm, passages_hbm, out_ref, len_out, queries_ref, passages_ref, sems,
    *, distance, block_size, rows, columns
):
    passage_count, token_count, _ = passages_hbm.shape
    size = out_ref.shape[0]
    per_dot = rows // token_count
    first = (lax.axis_index("gz") ^ distance) * block_size
    copies = [
        pltpu.make_async_copy(len_hbm, len_out, sems.at[0]),
        pltpu.make_async_copy(queries_hbm, queries_ref, sems.at[1]),
    ]
    for m in range(passage_count // per_dot):
        place = lax.rem(first + m * per_dot, passage_count)
        copies.append(
            pltpu.make_async_copy(
                passages_hbm.at[pl.ds(place, per_dot)], passages_ref.at[pl.ds(place, per_dot)], sems.at[2 + m]
            )
        )
    for copy in copies:
        copy.start()
    copies[0].wait()
    copies[1].wait()
    for m in range(size // per_dot):
        copies[2 + m].wait()
        best_tokens(
            len_out, queries_ref, passages_ref, out_ref, first + m * per_dot, m * per_dot, rows, columns
        )
    for copy in copies[2 + size // per_dot :]:
        copy.wait()


def maxima_kernel(len_ref, queries_ref, passages_ref, out_ref, *, distance, block_size, offset, rows, columns):
    first = (lax.axis_index("gz") ^ distance) * block_size + offset
    per_dot = rows // passages_ref.shape[1]
    for m in range(out_ref.shape[0] // per_dot):
        best_tokens(
            len_ref, queries_ref, passages_ref, out_ref, first + m * per_dot, m * per_dot, rows, columns
        )


def maxima(flat_queries, passages, passage_len, distance, block_size, offset, size, fill=False):
    passage_count, token_count, width = passages.shape
    query_rows = flat_queries.shape[0]
    per_dot = min(size, max(1, 1024 // token_count))
    settings = dict(
        distance=distance,
        block_size=block_size,
        rows=per_dot * token_count,
        columns=min(256, query_rows),
    )
    result = jax.ShapeDtypeStruct((size, query_rows), jnp.float32)
    smem, vmem = pl.BlockSpec(memory_space=pltpu.SMEM), pl.BlockSpec(memory_space=pltpu.VMEM)
    common = dict(
        cost_estimate=pl.CostEstimate(
            flops=2 * 2 * size * token_count * query_rows * width,
            bytes_accessed=size * (token_count * width * 2 + query_rows * 4),
            transcendentals=0,
        ),
        compiler_params=pltpu.CompilerParams(vmem_limit_bytes=14 * mebibyte),
        name=f"maxima_{distance}_{offset}",
    )
    operands = (passage_len, flat_queries, passages)
    if fill:
        return pl.pallas_call(
            functools.partial(first_kernel, **settings),
            in_specs=[pl.BlockSpec(memory_space=pltpu.HBM)] * 3,
            out_specs=[vmem, smem, vmem, vmem],
            out_shape=[result, *(jax.ShapeDtypeStruct(x.shape, x.dtype) for x in operands)],
            scratch_shapes=[pltpu.SemaphoreType.DMA((2 + passage_count // per_dot,))],
            **common,
        )(*operands)
    return pl.pallas_call(
        functools.partial(maxima_kernel, offset=offset, **settings),
        in_specs=[smem, vmem, vmem],
        out_specs=vmem,
        out_shape=result,
        **common,
    )(*operands)


def merge_kernel(*refs):
    *part_refs, len_ref, out_ref = refs
    query_count = out_ref.shape[1]
    lanes = part_refs[0].shape[1]
    query_rows = lanes // query_count
    merged = functools.reduce(jnp.maximum, [part[...] for part in part_refs])
    shape = (lanes, query_count)
    row = lax.broadcasted_iota(jnp.int32, shape, 0)
    start = lax.broadcasted_iota(jnp.int32, shape, 1) * query_rows
    used = jnp.clip(len_ref[...] - lax.axis_index("gy") * query_rows, 0, query_rows)
    counted = jnp.where((row >= start) & (row < start + used), 1.0, 0.0).astype(jnp.bfloat16)
    total = None
    for _ in range(3):
        piece = merged.astype(jnp.bfloat16)
        merged = merged - piece.astype(jnp.float32)
        term = jnp.dot(piece, counted, preferred_element_type=jnp.float32)
        total = term if total is None else total + term
    out_ref[...] = total


def merge(parts, query_len):
    query_count = query_len.shape[0]
    block_size = parts[0].shape[0]
    return pl.pallas_call(
        merge_kernel,
        out_shape=jax.ShapeDtypeStruct((block_size, query_count), jnp.float32),
        compiler_params=pltpu.CompilerParams(vmem_limit_bytes=12 * mebibyte),
        name="merge",
    )(*parts, query_len.reshape(1, query_count))


def exchange(array, axis, distance):
    size = lax.axis_size(axis)
    return lax.ppermute(array, axis, [(k, k ^ distance) for k in range(size)])


def hypercube(array, axis, combine):
    distance = 1
    while distance < lax.axis_size(axis):
        array = combine(array, exchange(array, axis, distance))
        distance *= 2
    return array


def join_pairs(one, other):
    top = jnp.maximum(one[0], other[0])
    summed = one[1] * jnp.exp(one[0] - top) + other[1] * jnp.exp(other[0] - top)
    return jnp.stack([top, summed])


def owned_maxima(score, start, block_size, owners):
    if owners != 4:
        size = start.shape[0]
        rest = [score(owners - 1, size, block_size - size)] if size < block_size else []
        sent = jnp.concatenate([start, *rest])
        return [exchange(sent, "gz", owners - 1)] + [
            exchange(score(distance, 0, block_size), "gz", distance) if distance else score(0, 0, block_size)
            for distance in range(owners - 2, -1, -1)
        ]
    half = start.shape[0]
    rest = block_size - half
    near = [named_exchange(start, 1), named_exchange(score(3, half, rest), 1)]
    far_0 = named_exchange(jnp.maximum(score(2, 0, half), near[0]), 2)
    beside = named_exchange(score(1, 0, block_size), 1)
    far_1 = named_exchange(jnp.maximum(score(2, half, rest), near[1]), 2)
    return [score(0, 0, block_size), beside, jnp.concatenate([far_0, far_1])]


def named_exchange(array, distance):
    return exchange(array, "gz", distance)


def shards(queries, passages, passage_len, query_len):
    query_count, query_rows, width = queries.shape
    passage_count = passages.shape[0]
    owners = lax.axis_size("gz")
    block_size = passage_count // owners
    flat_queries = queries.reshape(query_count * query_rows, width)
    flat_queries, passages, passage_len = (
        pltpu.with_memory_space_constraint(x, pltpu.HBM) for x in (flat_queries, passages, passage_len)
    )
    start, lengths, held_queries, held = maxima(
        flat_queries, passages, passage_len, owners - 1, block_size, 0, block_size // 2, fill=True
    )
    held = pltpu.with_memory_space_constraint(held, pltpu.VMEM)
    held_queries = pltpu.with_memory_space_constraint(held_queries, pltpu.VMEM)

    def score(distance, offset, size):
        return maxima(held_queries, held, lengths, distance, block_size, offset, size)

    partial_value = merge(owned_maxima(score, start, block_size, owners), query_len)
    scores = hypercube(partial_value, "gy", jnp.add)
    top = jnp.max(scores, axis=0)
    summed = jnp.sum(jnp.exp(scores - top[None]), axis=0)
    pair = hypercube(jnp.stack([top, summed]), "gx", join_pairs)
    pair = hypercube(pair, "gz", join_pairs)
    return jnp.transpose(scores - (pair[0] + jnp.log(pair[1]))[None])


def solution(mesh):
    return jax.shard_map(
        shards,
        mesh=mesh,
        in_specs=(P(None, "gy", None), P("gx", "gz", None), P("gx"), P()),
        out_specs=P(None, ("gx", "gz")),
        check_vma=False,
    )
```

time: 72 us -> 69 us (0.958)
  local copies, waits for them, and re-layouts: 5.75 us -> 0.74 us
  Pallas kernels: 22.4 us -> 24.5 us
    unnamed x8 -> x2, local copies, waits for them, and re-layouts: 5.02 us -> 0.01 us
    pallas_call x6, Pallas kernels: 21.9 us -> 24 us  [the longest x5 19.2 us: maxima(): pl.pallas_call(functools.partial(maxima_kernel, offset=offset, **settings...]
  transfers between devices with their start and end apart: 10 -> 10, of which waited for: 7 -> 7; matrix products, arithmetic and copies ran while one was open for 0% -> 0% of each run, Pallas kernels for 26% -> 24%
where the time goes in v3:
time: 69 us; the launch traced here: 68.8 us
  waiting for transfers between devices  30.5 us (44%)
  Pallas kernels  24.5 us (36%)
  starting transfers between devices  12.6 us (18%)
  local copies, waits for them, and re-layouts  0.74 us (1%)
    ppermute x10, waiting for transfers between devices, exchange(): return lax.ppermute(array, axis, [(k, k ^ distance) for k in range(size)])  30.5 us
    pallas_call x5, Pallas kernels, maxima(): pl.pallas_call(functools.partial(maxima_kernel, offset=offset, **settings...  19.2 us
    ppermute x10, starting transfers between devices, exchange(): return lax.ppermute(array, axis, [(k, k ^ distance) for k in range(size)])  12.6 us
    pallas_call x1, Pallas kernels, maxima(): pl.pallas_call(functools.partial(first_kernel, **settings), in_specs=[pl....  4.87 us
  transfers between devices with their start and end apart: 10, of which 7 were waited for; matrix products, arithmetic and copies ran while one was open for 0% of the time, Pallas kernels for 24%

profile of v3, /device:TPU:0, one launch (start us, length us, event | category | flops | bytes accessed | tf_op | source)
XLA Modules:
  0.0 68.8 jit_solution(433784426898427069)
XLA Ops:
  0.0 4.9 %maxima_3_0.1 = (f32[64,1024]{1,0:T(8,128)S(1)}, s32[512]{0:T(512)S(1)}, bf16[1024,128]{1,0:T(8,128)(2,1)S(1)}, bf16[512,64,128]{2,1,0:T(8,128)(2,1)S(1)}) custom-call(s32[512]{0:T(512)} %len_hbm.1, bf16[1024,128]{1,0:T(8,128)(2,1)} %bitcast.13, bf16[512,64,128]{2,1,0:T(8,128)(2,1)} %passages_hbm.1), custom_call_target="tpu_custom_call" | custom-call | flops 2147483648 | bytes 1310720 | tf_op jit(solution)/shard_map/maxima_3_0/pallas_call | solution.py:101
  4.9 2.9 %maxima_3_64.1 = f32[64,1024]{1,0:T(8,128)S(1)} custom-call(s32[512]{0:T(512)S(1)} %get-tuple-element.9.len_ref, bf16[1024,128]{1,0:T(8,128)(2,1)S(1)} %get-tuple-element.10.queries_ref, bf16[512,64,128]{2,1,0:T(8,128)(2,1)S(1)} %get-tuple-element.11.passages_ref), custom_call_target="tpu_custom_call" | custom-call | flops 2147483648 | bytes 1310720 | tf_op jit(solution)/shard_map/maxima_3_64/pallas_call | solution.py:109
  7.8 3.1 %collective-permute-start.3 = (f32[64,1024]{1,0:T(8,128)S(1)}, f32[64,1024]{1,0:T(8,128)S(1)}, u32[]{:S(2)}, u32[]{:S(2)}) collective-permute-start(f32[64,1024]{1,0:T(8,128)S(1)} %maxima_3_64.1), channel_id=1, source_target_pairs={{0,1},{1,0},{2,3},{3,2},{4,5},{5,4},{6,7},{7,6},{8,9},{9,8},{10,11... | collective-permute-start | bytes 786440 | tf_op jit(solution)/shard_map/ppermute | solution.py:151
  10.9 0.1 collective-permute-start.1
  11.0 5.1 %maxima_1_0.1 = f32[128,1024]{1,0:T(8,128)S(1)} custom-call(s32[512]{0:T(512)S(1)} %get-tuple-element.9.len_ref, bf16[1024,128]{1,0:T(8,128)(2,1)S(1)} %get-tuple-element.10.queries_ref, bf16[512,64,128]{2,1,0:T(8,128)(2,1)S(1)} %get-tuple-element.11.passages_ref), custom_call_target="tpu_custom_call" | custom-call | flops 4294967296 | bytes 2621440 | tf_op jit(solution)/shard_map/maxima_1_0/pallas_call | solution.py:109
  16.1 2.0 %collective-permute-start = (f32[128,1024]{1,0:T(8,128)S(1)}, f32[128,1024]{1,0:T(8,128)S(1)}, u32[]{:S(2)}, u32[]{:S(2)}) collective-permute-start(f32[128,1024]{1,0:T(8,128)S(1)} %maxima_1_0.1), channel_id=1, source_target_pairs={{0,1},{1,0},{2,3},{3,2},{4,5},{5,4},{6,7},{7,6},{8,9},{9,8},{10,11... | collective-permute-start | bytes 1572872 | tf_op jit(solution)/shard_map/ppermute | solution.py:151
  18.1 3.1 %maxima_2_64.1 = f32[64,1024]{1,0:T(8,128)S(1)} custom-call(s32[512]{0:T(512)S(1)} %get-tuple-element.9.len_ref, bf16[1024,128]{1,0:T(8,128)(2,1)S(1)} %get-tuple-element.10.queries_ref, bf16[512,64,128]{2,1,0:T(8,128)(2,1)S(1)} %get-tuple-element.11.passages_ref), custom_call_target="tpu_custom_call" | custom-call | flops 2147483648 | bytes 1310720 | tf_op jit(solution)/shard_map/maxima_2_64/pallas_call | solution.py:109
  21.3 2.9 %maxima_2_0.1 = f32[64,1024]{1,0:T(8,128)S(1)} custom-call(s32[512]{0:T(512)S(1)} %get-tuple-element.9.len_ref, bf16[1024,128]{1,0:T(8,128)(2,1)S(1)} %get-tuple-element.10.queries_ref, bf16[512,64,128]{2,1,0:T(8,128)(2,1)S(1)} %get-tuple-element.11.passages_ref), custom_call_target="tpu_custom_call" | custom-call | flops 2147483648 | bytes 1310720 | tf_op jit(solution)/shard_map/maxima_2_0/pallas_call | solution.py:109
  24.2 0.0 collective-permute-done.3
  24.2 2.7 %collective-permute-start.4 = (f32[64,1024]{1,0:T(8,128)S(1)}, f32[64,1024]{1,0:T(8,128)S(1)}, u32[]{:S(2)}, u32[]{:S(2)}) collective-permute-start(f32[64,1024]{1,0:T(8,128)S(1)} %max.25), channel_id=1, source_target_pairs={{0,2},{1,3},{2,0},{3,1},{4,6},{5,7},{6,4},{7,5},{8,10},{9,11},{10,... | collective-permute-start | bytes 786440 | tf_op jit(solution)/shard_map/ppermute | solution.py:151
  26.9 0.0 collective-permute-done.1
  26.9 0.0 copy-start
  27.0 0.4 collective-permute-start.2
  27.4 5.1 %maxima_0_0.1.refs_0_ = f32[128,1024]{1,0:T(8,128)S(1)} custom-call(s32[512]{0:T(512)S(1)} %get-tuple-element.9.len_ref, bf16[1024,128]{1,0:T(8,128)(2,1)S(1)} %get-tuple-element.10.queries_ref, bf16[512,64,128]{2,1,0:T(8,128)(2,1)S(1)} %get-tuple-element.11.passages_ref), custom_call_target="tpu_custom_call" | custom-call | flops 4294967296 | bytes 2621440 | tf_op jit(solution)/shard_map/maxima_0_0/pallas_call | solution.py:109
  32.5 7.7 %collective-permute-done.4 = f32[64,1024]{1,0:T(8,128)S(1)} collective-permute-done((f32[64,1024]{1,0:T(8,128)S(1)}, f32[64,1024]{1,0:T(8,128)S(1)}, u32[]{:S(2)}, u32[]{:S(2)}) %collective-permute-start.4) | collective-permute-done | bytes 262176 | tf_op jit(solution)/shard_map/ppermute | solution.py:151
  40.1 9.2 %collective-permute-done.2 = f32[64,1024]{1,0:T(8,128)S(1)} collective-permute-done((f32[64,1024]{1,0:T(8,128)S(1)}, f32[64,1024]{1,0:T(8,128)S(1)}, u32[]{:S(2)}, u32[]{:S(2)}) %collective-permute-start.2) | collective-permute-done | bytes 262176 | tf_op jit(solution)/shard_map/ppermute | solution.py:151
  49.3 0.0 collective-permute-done.refs_1_
  49.4 0.0 copy-done
  49.4 0.5 merge.1
  49.9 1.6 %collective-permute-start.5 = (f32[128,128]{1,0:T(8,128)S(1)}, f32[128,128]{1,0:T(8,128)S(1)}, u32[]{:S(2)}, u32[]{:S(2)}) collective-permute-start(f32[128,128]{1,0:T(8,128)S(1)} %merge.1), channel_id=1, source_target_pairs={{0,4},{4,0},{8,12},{12,8},{1,5},{5,1},{9,13},{13,9},{2,6},{6,2},{1... | collective-permute-start | bytes 196616 | tf_op jit(solution)/shard_map/ppermute | solution.py:151
  51.4 2.8 %collective-permute-done.5 = f32[128,128]{1,0:T(8,128)S(1)} collective-permute-done((f32[128,128]{1,0:T(8,128)S(1)}, f32[128,128]{1,0:T(8,128)S(1)}, u32[]{:S(2)}, u32[]{:S(2)}) %collective-permute-start.5) | collective-permute-done | bytes 65568 | tf_op jit(solution)/shard_map/ppermute | solution.py:151
  54.2 1.6 %collective-permute-start.6 = (f32[128,128]{1,0:T(8,128)S(1)}, f32[128,128]{1,0:T(8,128)S(1)}, u32[]{:S(2)}, u32[]{:S(2)}) collective-permute-start(f32[128,128]{1,0:T(8,128)S(1)} %add.25), channel_id=1, source_target_pairs={{0,8},{4,12},{8,0},{12,4},{1,9},{5,13},{9,1},{13,5},{2,10},{6,14},... | collective-permute-start | bytes 196616 | tf_op jit(solution)/shard_map/ppermute | solution.py:151
  55.8 2.7 %collective-permute-done.6 = f32[128,128]{1,0:T(8,128)S(1)} collective-permute-done((f32[128,128]{1,0:T(8,128)S(1)}, f32[128,128]{1,0:T(8,128)S(1)}, u32[]{:S(2)}, u32[]{:S(2)}) %collective-permute-start.6) | collective-permute-done | bytes 65568 | tf_op jit(solution)/shard_map/ppermute | solution.py:151
  58.6 0.1 collective-permute-start.7
  58.7 1.1 %collective-permute-done.7 = f32[2,128]{1,0:T(2,128)S(1)} collective-permute-done((f32[2,128]{1,0:T(2,128)S(1)}, f32[2,128]{1,0:T(2,128)S(1)}, u32[]{:S(2)}, u32[]{:S(2)}) %collective-permute-start.7) | collective-permute-done | bytes 1056 | tf_op jit(solution)/shard_map/ppermute | solution.py:151
  59.9 0.1 collective-permute-start.8
  60.0 3.6 %collective-permute-done.8 = f32[2,128]{1,0:T(2,128)S(1)} collective-permute-done((f32[2,128]{1,0:T(2,128)S(1)}, f32[2,128]{1,0:T(2,128)S(1)}, u32[]{:S(2)}, u32[]{:S(2)}) %collective-permute-start.8) | collective-permute-done | bytes 1056 | tf_op jit(solution)/shard_map/ppermute | solution.py:151
  63.5 1.1 %collective-permute-start.9 = (f32[2,128]{1,0:T(2,128)S(1)}, f32[2,128]{1,0:T(2,128)S(1)}, u32[]{:S(2)}, u32[]{:S(2)}) collective-permute-start(f32[2,128]{1,0:T(2,128)S(1)} %pad_maximum_fusion.3), channel_id=1, source_target_pairs={{0,2},{1,3},{2,0},{3,1},{4,6},{5,7},{6,4},{7,5},{8,10},{9,11},{10,... | collective-permute-start | bytes 3080 | tf_op jit(solution)/shard_map/ppermute | solution.py:151
  64.6 3.5 %collective-permute-done.9 = f32[2,128]{1,0:T(2,128)S(1)} collective-permute-done((f32[2,128]{1,0:T(2,128)S(1)}, f32[2,128]{1,0:T(2,128)S(1)}, u32[]{:S(2)}, u32[]{:S(2)}) %collective-permute-start.9) | collective-permute-done | bytes 1056 | tf_op jit(solution)/shard_map/ppermute | solution.py:151
  68.1 0.7 %copy.5 = f32[128,128]{1,0:T(8,128)} copy(f32[128,128]{0,1:T(8,128)S(1)} %subtract_bitcast_fusion) | data formatting | bytes 131072 | tf_op jit(solution)/shard_map/transpose | solution.py:214
  (13 shorter events, 0.3 us)
Async XLA Ops:
  7.8 16.4 %collective-permute-start.3 = (f32[64,1024]{1,0:T(8,128)S(1)}, f32[64,1024]{1,0:T(8,128)S(1)}, u32[]{:S(2)}, u32[]{:S(2)}) collective-permute-start(f32[64,1024]{1,0:T(8,128)S(1)} %maxima_3_64.1), channel_id=1, source_target_pairs={{0,1},{1,0},{2,3},{3,2},{4,5},{5,4},{6,7},{7,6},{8,9},{9,8},{10,11... | collective-permute-start | bytes 786440 | tf_op jit(solution)/shard_map/ppermute | solution.py:151
  10.9 16.0 %collective-permute-start.1 = (f32[64,1024]{1,0:T(8,128)S(1)}, f32[64,1024]{1,0:T(8,128)S(1)}, u32[]{:S(2)}, u32[]{:S(2)}) collective-permute-start(f32[64,1024]{1,0:T(8,128)S(1)} %get-tuple-element.12), channel_id=1, source_target_pairs={{0,1},{1,0},{2,3},{3,2},{4,5},{5,4},{6,7},{7,6},{8,9},{9,8},{10,11... | collective-permute-start | bytes 786440 | tf_op jit(solution)/shard_map/ppermute | solution.py:151
  16.1 33.2 %collective-permute-start = (f32[128,1024]{1,0:T(8,128)S(1)}, f32[128,1024]{1,0:T(8,128)S(1)}, u32[]{:S(2)}, u32[]{:S(2)}) collective-permute-start(f32[128,1024]{1,0:T(8,128)S(1)} %maxima_1_0.1), channel_id=1, source_target_pairs={{0,1},{1,0},{2,3},{3,2},{4,5},{5,4},{6,7},{7,6},{8,9},{9,8},{10,11... | collective-permute-start | bytes 1572872 | tf_op jit(solution)/shard_map/ppermute | solution.py:151
  24.2 15.9 %collective-permute-start.4 = (f32[64,1024]{1,0:T(8,128)S(1)}, f32[64,1024]{1,0:T(8,128)S(1)}, u32[]{:S(2)}, u32[]{:S(2)}) collective-permute-start(f32[64,1024]{1,0:T(8,128)S(1)} %max.25), channel_id=1, source_target_pairs={{0,2},{1,3},{2,0},{3,1},{4,6},{5,7},{6,4},{7,5},{8,10},{9,11},{10,... | collective-permute-start | bytes 786440 | tf_op jit(solution)/shard_map/ppermute | solution.py:151
  26.9 22.4 %copy-start = (s32[128]{0:T(128)S(1)}, s32[128]{0:T(128)}, u32[]{:S(2)}) copy-start(s32[128]{0:T(128)} %param.7) | copy-start | bytes 1540
  27.0 22.4 %collective-permute-start.2 = (f32[64,1024]{1,0:T(8,128)S(1)}, f32[64,1024]{1,0:T(8,128)S(1)}, u32[]{:S(2)}, u32[]{:S(2)}) collective-permute-start(f32[64,1024]{1,0:T(8,128)S(1)} %max.24), channel_id=1, source_target_pairs={{0,2},{1,3},{2,0},{3,1},{4,6},{5,7},{6,4},{7,5},{8,10},{9,11},{10,... | collective-permute-start | bytes 786440 | tf_op jit(solution)/shard_map/ppermute | solution.py:151
  49.9 4.3 %collective-permute-start.5 = (f32[128,128]{1,0:T(8,128)S(1)}, f32[128,128]{1,0:T(8,128)S(1)}, u32[]{:S(2)}, u32[]{:S(2)}) collective-permute-start(f32[128,128]{1,0:T(8,128)S(1)} %merge.1), channel_id=1, source_target_pairs={{0,4},{4,0},{8,12},{12,8},{1,5},{5,1},{9,13},{13,9},{2,6},{6,2},{1... | collective-permute-start | bytes 196616 | tf_op jit(solution)/shard_map/ppermute | solution.py:151
  54.2 4.3 %collective-permute-start.6 = (f32[128,128]{1,0:T(8,128)S(1)}, f32[128,128]{1,0:T(8,128)S(1)}, u32[]{:S(2)}, u32[]{:S(2)}) collective-permute-start(f32[128,128]{1,0:T(8,128)S(1)} %add.25), channel_id=1, source_target_pairs={{0,8},{4,12},{8,0},{12,4},{1,9},{5,13},{9,1},{13,5},{2,10},{6,14},... | collective-permute-start | bytes 196616 | tf_op jit(solution)/shard_map/ppermute | solution.py:151
  58.6 1.2 %collective-permute-start.7 = (f32[2,128]{1,0:T(2,128)S(1)}, f32[2,128]{1,0:T(2,128)S(1)}, u32[]{:S(2)}, u32[]{:S(2)}) collective-permute-start(f32[2,128]{1,0:T(2,128)S(1)} %pad_maximum_fusion.1), channel_id=1, source_target_pairs={{0,16},{16,0},{1,17},{17,1},{2,18},{18,2},{3,19},{19,3},{4,20},{20... | collective-permute-start | bytes 3080 | tf_op jit(solution)/shard_map/ppermute | solution.py:151
  59.9 3.6 %collective-permute-start.8 = (f32[2,128]{1,0:T(2,128)S(1)}, f32[2,128]{1,0:T(2,128)S(1)}, u32[]{:S(2)}, u32[]{:S(2)}) collective-permute-start(f32[2,128]{1,0:T(2,128)S(1)} %pad_maximum_fusion.2), channel_id=1, source_target_pairs={{0,1},{1,0},{2,3},{3,2},{4,5},{5,4},{6,7},{7,6},{8,9},{9,8},{10,11... | collective-permute-start | bytes 3080 | tf_op jit(solution)/shard_map/ppermute | solution.py:151
  63.5 4.5 %collective-permute-start.9 = (f32[2,128]{1,0:T(2,128)S(1)}, f32[2,128]{1,0:T(2,128)S(1)}, u32[]{:S(2)}, u32[]{:S(2)}) collective-permute-start(f32[2,128]{1,0:T(2,128)S(1)} %pad_maximum_fusion.3), channel_id=1, source_target_pairs={{0,2},{1,3},{2,0},{3,1},{4,6},{5,7},{6,4},{7,5},{8,10},{9,11},{10,... | collective-permute-start | bytes 3080 | tf_op jit(solution)/shard_map/ppermute | solution.py:151
